TPU v7x, 32 devices: a whole 2x2x4 slice. The times are simulated.
32 devices in a mesh: node: 8 (over z, y), local: 4 (over x, core).
Axes of the slice: x: 2, y: 2, z: 4, core: 2. Of those that a mesh axis runs over, the one named last changes fastest.
Arguments:
- tokens: bfloat16 [4096, 4096], P(('node', 'local')), may hold values from -6 to 6
- expert_ids: int32 [4096, 8], P(('node', 'local')), may hold values from 0 to 31, all different within a row; in each aligned block of 128 rows (0 to 127, 128 to 255, ...) at most 40 rows name the same one
- gate_scores: float32 [4096, 8], P(('node', 'local')), may hold values from 0.03 to 0.4
- w_gate: bfloat16 [32, 4096, 768], P(('node', 'local')), may hold values from -0.09375 to 0.09375
- w_up: bfloat16 [32, 4096, 768], P(('node', 'local')), may hold values from -0.09375 to 0.09375
- w_down: bfloat16 [32, 768, 4096], P(('node', 'local')), may hold values from -0.21875 to 0.21875
Outputs:
- mixed: bfloat16 [4096, 4096], P(('node', 'local'))
Inputs may be any that keep to these rules, and one draw needn't show every extreme that they name: `expert_ids`: each row names 8 different experts. Among the 128 rows of one device no expert is named more than 40 times, and that many is reached on some device.
All inputs are finite; a program needn't handle non-finite values.
Results may differ from a plain program's by a relative error of at most 0.0058.
Values may be sent and summed in bfloat16 or wider, within the bound.
No kernel may reach another device: no remote copies, remote signals or barrier semaphores. Data moves between devices by JAX's collectives and lax.ppermute only.
A program may use at most 128 MiB of HBM per device.

v0:
```python
import jax
import jax.numpy as jnp
from jax import lax
from jax.sharding import PartitionSpec as P


def per_device(tokens, expert_ids, gate_scores, w_gate, w_up, w_down):
    node_count = lax.axis_size("node")
    local_count = lax.axis_size("local")
    experts = node_count * local_count
    token_count = tokens.shape[0]
    features = tokens.shape[1]
    top_count = expert_ids.shape[1]
    capacity = 5 * token_count * top_count // (4 * experts)
    flat_ids = expert_ids.reshape(-1)
    onehot = (flat_ids[:, None] == jnp.arange(experts, dtype=jnp.int32)[None, :]).astype(jnp.int32)
    before = jnp.cumsum(onehot, axis=0) - onehot
    slot_rank = jnp.sum(before * onehot, axis=1)
    slot_index = flat_ids * capacity + slot_rank
    source = jnp.arange(token_count * top_count, dtype=jnp.int32) // top_count
    packed = (
        jnp.zeros((experts * capacity, features), jnp.bfloat16).at[slot_index].set(tokens[source])
    )
    received = lax.all_to_all(
        packed.reshape(experts, capacity, features),
        ("node", "local"),
        split_axis=0,
        concat_axis=0,
        tiled=True,
    )
    in_shape = received.shape
    flat_in = received.reshape(-1, in_shape[-1])
    gate_part = jnp.dot(flat_in, w_gate[0], preferred_element_type=jnp.float32)
    up_part = jnp.dot(flat_in, w_up[0], preferred_element_type=jnp.float32)
    hidden = (jax.nn.silu(gate_part) * up_part).astype(jnp.bfloat16)
    output = jnp.dot(hidden, w_down[0], preferred_element_type=jnp.float32).astype(jnp.bfloat16)
    returned_rows = lax.all_to_all(
        output.reshape(in_shape), ("node", "local"), split_axis=0, concat_axis=0, tiled=True
    )
    returned_rows = returned_rows.reshape(experts * capacity, features)
    picked = returned_rows[slot_index].astype(jnp.float32)
    weighted = picked.reshape(token_count, top_count, features) * gate_scores[:, :, None]
    return jnp.sum(weighted, axis=1).astype(jnp.bfloat16)


def solution(mesh):
    in_specs = (
        P(("node", "local"), None),
        P(("node", "local"), None),
        P(("node", "local"), None),
        P(("node", "local"), None, None),
        P(("node", "local"), None, None),
        P(("node", "local"), None, None),
    )
    out_specs = P(("node", "local"), None)
    return jax.shard_map(
        per_device, mesh=mesh, in_specs=in_specs, out_specs=out_specs, check_vma=False
    )
```

profile of v0, /device:TPU:0, one launch (start us, length us, event | category | flops | bytes accessed | tf_op | source)
XLA Modules:
  0.0 576.2 jit_solution(39341286932561640)
XLA Ops:
  0.0 0.0 copy-start
  0.0 0.9 copy.9
  0.9 0.1 eq.29
  1.0 0.1 eq.25
  1.1 0.7 broadcast_multiply_fusion
  1.8 9.0 %reduce-window.6 = s32[32,8,128]{2,1,0:T(8,128)S(1)} reduce-window(s32[32,8,128]{2,1,0:T(8,128)S(1)} %fusion.17, s32[]{:T(128)} %constant.28.clone.1), window={size=1x1x128 pad=0_0x0_0x127_0}, to_apply=%region_0.0 | reduce-window | flops 4161536 | bytes 262148 | tf_op jit(solution)/shard_map/reduce-window
  10.8 0.1 slice.12
  10.9 0.1 copy.11
  11.1 0.1 copy.12
  11.1 0.1 broadcast_add_fusion
  11.3 0.1 copy.8
  11.4 0.1 mul.36
  11.5 0.0 copy-done
  11.5 7.8 %gather_fusion = bf16[1024,4096]{1,0:T(8,128)(2,1)} fusion(bf16[128,4096]{1,0:T(8,128)(2,1)S(1)} %copy-done, s32[1024]{0:T(1024)S(1)} %broadcast_clamp_fusion.1), kind=kCustom, calls=%fused_computation | custom fusion | bytes 16781312 | tf_op jit(solution)/shard_map/gather | solution.py:22
  19.3 18.8 %scatter_custom_fusion = bf16[1280,4096]{1,0:T(8,128)(2,1)} fusion(s32[1024]{0:T(1024)S(1)} %bitcast.51, bf16[1024,4096]{1,0:T(8,128)(2,1)} %gather_fusion, bf16[]{:T(256)} %constant.26.clone.1), kind=kCustom, calls=%fused_computation.11 | custom fusion | bytes 10486272 | tf_op jit(solution)/shard_map/scatter | solution.py:22
  38.2 0.0 slice-start
  38.2 0.0 slice-start.2
  38.2 235.8 %all_to_all.10 = bf16[32,40,4096]{2,1,0:T(8,128)(2,1)S(1)} all-to-all(bf16[32,40,4096]{2,1,0:T(8,128)(2,1)} %bitcast.44), channel_id=1, replica_groups=mesh['node'=8,'local'=4] {'node','local'}, dimensions={0} | all-to-all | bytes 20971520 | tf_op jit(solution)/shard_map/all_to_all | solution.py:24
  273.9 11.8 %fusion.4 = f32[1280,768]{1,0:T(8,128)} fusion(bf16[1280,4096]{1,0:T(8,128)(2,1)S(1)} %bitcast.46, bf16[1,4096,768]{2,1,0:T(8,128)(2,1)} %param.9), kind=kOutput, calls=%fused_computation.9 | convolution fusion | flops 8053063680 | bytes 20709376 | tf_op jit(solution)/shard_map/dot_general | solution.py:33
  285.8 0.0 slice-done
  285.8 0.0 slice-done.1
  285.8 10.3 %fusion.11 = bf16[1280,768]{1,0:T(8,128)(2,1)S(1)} fusion(bf16[1280,4096]{1,0:T(8,128)(2,1)S(1)} %bitcast.47, bf16[1,4096,768]{2,1,0:T(8,128)(2,1)S(1)} %bitcast.55, f32[1280,768]{1,0:T(8,128)} %fusion.4), kind=kOutput, calls=%fused_computation.14 | convolution fusion | flops 8058961920 | bytes 22675456 | tf_op jit(solution)/shard_map/dot_general | solution.py:34
  296.1 0.0 slice-done.2
  296.1 0.0 slice-done.3
  296.1 10.6 %convolution_convert_fusion = bf16[1280,4096]{1,0:T(8,128)(2,1)} fusion(bf16[1280,768]{1,0:T(8,128)(2,1)S(1)} %fusion.11, bf16[1,768,4096]{2,1,0:T(8,128)(2,1)S(1)} %bitcast.57), kind=kOutput, calls=%fused_computation.5 | convolution fusion | flops 8058306560 | bytes 18743296 | tf_op jit(solution)/shard_map/dot_general | solution.py:36
  306.7 4.1 all-to-all-start.1
  310.8 0.0 copy-done.2
  310.8 0.1 copy.13
  310.9 231.8 %all-to-all-done.1 = bf16[32,40,4096]{2,1,0:T(8,128)(2,1)} async-done(((bf16[32,40,4096]{2,1,0:T(8,128)(2,1)}), bf16[32,40,4096]{2,1,0:T(8,128)(2,1)}, u32[]{:S(2)}, u32[]{:S(2)}) %all-to-all-start.1) | async-done | bytes 10485792 | tf_op jit(solution)/shard_map/all_to_all | solution.py:37
  542.7 20.5 %gather_fusion.1 = bf16[1024,4096]{1,0:T(8,128)(2,1)} fusion(bf16[1280,4096]{1,0:T(8,128)(2,1)} %bitcast.11, s32[1024]{0:T(1024)S(1)} %broadcast_clamp_fusion), kind=kCustom, calls=%fused_computation.1 | custom fusion | bytes 16781312 | tf_op jit(solution)/shard_map/gather | solution.py:41
  563.3 12.9 %fusion = bf16[128,4096]{1,0:T(8,128)(2,1)} fusion(bf16[1024,4096]{1,0:T(8,128)(2,1)} %gather_fusion.1, f32[128,8]{1,0:T(8,128)S(1)} %copy.13), kind=kLoop, calls=%fused_computation.4 | loop fusion | flops 12058624 | bytes 9441280 | tf_op jit(solution)/shard_map/reduce_sum | solution.py:43
  576.1 0.0 copy-done.1
  (14 shorter events, 0.1 us)
Async XLA Ops:
  0.0 11.5 %copy-start = (bf16[128,4096]{1,0:T(8,128)(2,1)S(1)}, bf16[128,4096]{1,0:T(8,128)(2,1)}, u32[]{:S(2)}) copy-start(bf16[128,4096]{1,0:T(8,128)(2,1)} %param.6) | copy-start | bytes 3145732
  38.2 247.6 %slice-start = ((s8[6291456]{0:T(1024)(128)(4,1)}), s8[4194304]{0:T(1024)(128)(4,1)S(1)}, s32[]{:S(2)}) async-start(s8[6291456]{0:T(1024)(128)(4,1)} %bitcast.54), calls=%async_computation.2 | async-start | bytes 8388608
  38.2 257.9 %slice-start.2 = ((s8[6291456]{0:T(1024)(128)(4,1)}), s8[4194304]{0:T(1024)(128)(4,1)S(1)}, s32[]{:S(2)}) async-start(s8[6291456]{0:T(1024)(128)(4,1)} %bitcast.56), calls=%async_computation.4 | async-start | bytes 8388608
  273.9 11.8 %slice-start.1 = ((s8[6291456]{0:T(1024)(128)(4,1)}), s8[2097152]{0:T(1024)(128)(4,1)S(1)}, s32[]{:S(2)}) async-start(s8[6291456]{0:T(1024)(128)(4,1)} %bitcast.54), calls=%async_computation.3 | async-start | bytes 4194304
  273.9 22.1 %slice-start.3 = ((s8[6291456]{0:T(1024)(128)(4,1)}), s8[2097152]{0:T(1024)(128)(4,1)S(1)}, s32[]{:S(2)}) async-start(s8[6291456]{0:T(1024)(128)(4,1)} %bitcast.56), calls=%async_computation.5 | async-start | bytes 4194304
  306.7 4.1 copy-start.2
  306.7 236.0 %all-to-all-start.1 = ((bf16[32,40,4096]{2,1,0:T(8,128)(2,1)}), bf16[32,40,4096]{2,1,0:T(8,128)(2,1)}, u32[]{:S(2)}, u32[]{:S(2)}) async-start(bf16[32,40,4096]{2,1,0:T(8,128)(2,1)} %bitcast.45), calls=%async_computation.1 | async-start | bytes 20971520 | tf_op jit(solution)/shard_map/all_to_all | solution.py:37
  542.7 33.4 %copy-start.1 = (bf16[128,4096]{1,0:T(8,128)(2,1)S(1)}, bf16[128,4096]{1,0:T(8,128)(2,1)}, u32[]{:S(2)}) copy-start(bf16[128,4096]{1,0:T(8,128)(2,1)} %param.6) | copy-start | bytes 3145732
where the time goes:
time: 576 us
  blocking collectives  236 us (41%)
  waiting for transfers between devices  232 us (40%)
  local copies, waits for them, and re-layouts  48.8 us (8%)
  matrix products  32.7 us (6%)
  other arithmetic  22.8 us (4%)
    all_to_all x1, blocking collectives, per_device(): lax.all_to_all(packed.reshape(experts, capacity, features), ('node', 'loc...  236 us
    all_to_all x1, waiting for transfers between devices, per_device(): lax.all_to_all(output.reshape(in_shape), ('node', 'local'), split_axis=0,...  232 us
    gather x1, local copies, waits for them, and re-layouts, per_device(): picked = returned_rows[slot_index].astype(jnp.float32)  20.5 us
    scatter x1, local copies, waits for them, and re-layouts, per_device(): jnp.zeros((experts * capacity, features), jnp.bfloat16).at[slot_index]  18.8 us
    reduce_sum x1, other arithmetic, per_device(): return jnp.sum(weighted, axis=1).astype(jnp.bfloat16)  12.9 us
    dot_general x1, matrix products, per_device(): gate_part = jnp.dot(flat_in, w_gate[0], preferred_element_type=jnp.float32)  11.8 us
  transfers between devices with their start and end apart: 1, of which 1 were waited for; matrix products, arithmetic and copies ran while one was open for 0% of the time, Pallas kernels for 0%

commit v1 on v0

v1 whole, which is shorter than its diff:
```python
import functools

import jax
import jax.numpy as jnp
import numpy as np
from jax import lax
from jax.experimental import pallas as pl
from jax.experimental.pallas import tpu as pltpu
from jax.sharding import PartitionSpec as P


AXES = ("node", "local")
BF16 = jnp.bfloat16
F32 = jnp.float32
COLUMN_STEPS = 4


def planes_of(mesh):
    flat = mesh.devices.reshape(-1)
    depth = np.array([getattr(d, "coords", (0, 0, 0))[2] for d in flat])
    count = len(set(depth.tolist()))
    rows = depth.reshape(count, -1) if flat.size % count == 0 else depth.reshape(1, -1)
    if count > 1 and all(len(set(r.tolist())) == 1 for r in rows):
        return count
    return 1


def picks(table, capacity):
    experts, count = table.shape
    slots = lax.broadcasted_iota(jnp.int32, (capacity, count), 0).astype(F32)
    return [table[e : e + 1, :] == slots for e in range(experts)]


def pack_kernel(capacity, facts_ref, rows_ref, *outs):
    experts = len(outs)
    chosen = jnp.concatenate(
        [jnp.where(r, 1.0, 0.0) for r in picks(facts_ref[:experts, :], capacity)], axis=0
    ).astype(BF16)
    packed = jnp.dot(chosen, rows_ref[...], preferred_element_type=F32).astype(BF16)
    for e, out in enumerate(outs):
        out[...] = packed[e * capacity : (e + 1) * capacity, :]


def pack(facts, rows, capacity):
    experts, (count, features) = facts.shape[0] // 2, rows.shape
    step = features // COLUMN_STEPS
    return pl.pallas_call(
        functools.partial(pack_kernel, capacity),
        grid=(COLUMN_STEPS,),
        in_specs=[
            pl.BlockSpec(facts.shape, lambda i: (0, 0)),
            pl.BlockSpec((count, step), lambda i: (0, i)),
        ],
        out_specs=[pl.BlockSpec((capacity, step), lambda i: (0, i))] * experts,
        out_shape=[jax.ShapeDtypeStruct((capacity, features), BF16)] * experts,
        cost_estimate=pl.CostEstimate(
            flops=2 * experts * capacity * count * features,
            bytes_accessed=2 * (experts * capacity + count) * features,
            transcendentals=0,
        ),
    )(facts, rows)


def mix_kernel(capacity, experts, facts_ref, *refs):
    *rows, out_ref = refs
    weight = jnp.concatenate(
        [
            jnp.where(r, facts_ref[experts + e : experts + e + 1, :], 0.0)
            for e, r in enumerate(picks(facts_ref[:experts, :], capacity))
        ],
        axis=0,
    )
    high = weight.astype(BF16)
    low = (weight - high.astype(F32)).astype(BF16)
    dims = (((0,), (0,)), ((), ()))
    value = jnp.concatenate([r[...] for r in rows[:experts]], axis=0)
    total = lax.dot_general(high, value, dims, preferred_element_type=F32)
    total += lax.dot_general(low, value, dims, preferred_element_type=F32)
    for other in rows[experts:]:
        total += other[...].astype(F32)
    out_ref[...] = total.astype(out_ref.dtype)


def mix(facts, rows, others, capacity):
    experts, count, features = facts.shape[0] // 2, facts.shape[1], rows[0].shape[1]
    step = features // COLUMN_STEPS
    tall = [pl.BlockSpec((r.shape[0], step), lambda i: (0, i)) for r in [*rows, *others]]
    return pl.pallas_call(
        functools.partial(mix_kernel, capacity, experts),
        grid=(COLUMN_STEPS,),
        in_specs=[pl.BlockSpec(facts.shape, lambda i: (0, 0)), *tall],
        out_specs=pl.BlockSpec((count, step), lambda i: (0, i)),
        out_shape=jax.ShapeDtypeStruct((count, features), BF16),
        cost_estimate=pl.CostEstimate(
            flops=4 * experts * capacity * count * features,
            bytes_accessed=2 * (experts * capacity + 2 * count) * features,
            transcendentals=0,
        ),
    )(facts, *rows, *others)


def ffn_kernel(pieces, capacity, gate_ref, up_ref, down_ref, *refs):
    rows, outs, (held, total) = refs[:pieces], refs[pieces : 2 * pieces], refs[2 * pieces :]
    step, last = pl.program_id(0), pl.num_programs(0) - 1

    @pl.when(step == 0)
    def _():
        for m in range(pieces):
            held[m * capacity : (m + 1) * capacity, :] = rows[m][...]

    value = held[...]
    gate_part = jnp.dot(value, gate_ref[0], preferred_element_type=F32)
    up_part = jnp.dot(value, up_ref[0], preferred_element_type=F32)
    hidden = (gate_part / (1.0 + jnp.exp(-gate_part)) * up_part).astype(BF16)
    part = jnp.dot(hidden, down_ref[0], preferred_element_type=F32)

    @pl.when(step == 0)
    def _():
        total[...] = part

    @pl.when((step > 0) & (step < last))
    def _():
        total[...] += part

    @pl.when((step > 0) & (step == last))
    def _():
        total[...] += part

    @pl.when(step == last)
    def _():
        for m in range(pieces):
            outs[m][...] = total[m * capacity : (m + 1) * capacity, :].astype(BF16)


def ffn(rows, w_gate, w_up, w_down):
    pieces, (capacity, features) = len(rows), rows[0].shape
    hidden = w_gate.shape[2]
    tile = 256 if hidden % 256 == 0 else hidden
    steps = hidden // tile
    whole = pl.BlockSpec((capacity, features), lambda i: (0, 0))
    count = pieces * capacity
    return pl.pallas_call(
        functools.partial(ffn_kernel, pieces, capacity),
        grid=(steps,),
        in_specs=[
            pl.BlockSpec((1, features, tile), lambda i: (0, 0, i)),
            pl.BlockSpec((1, features, tile), lambda i: (0, 0, i)),
            pl.BlockSpec((1, tile, features), lambda i: (0, i, 0)),
        ]
        + [whole] * pieces,
        out_specs=[whole] * pieces,
        out_shape=[jax.ShapeDtypeStruct((capacity, features), BF16)] * pieces,
        scratch_shapes=[
            pltpu.VMEM((count, features), BF16),
            pltpu.VMEM((count, features), F32),
        ],
        compiler_params=pltpu.CompilerParams(vmem_limit_bytes=56 * 1024 * 1024),
        cost_estimate=pl.CostEstimate(
            flops=6 * count * features * hidden,
            bytes_accessed=2 * features * (3 * hidden + 2 * count),
            transcendentals=count * hidden,
        ),
    )(w_gate, w_up, w_down, *rows)


def layer(planes, size, tokens, expert_ids, gate_scores, w_gate, w_up, w_down):
    width = size // planes
    token_count, _ = tokens.shape
    top_count = expert_ids.shape[1]
    capacity = 5 * token_count * top_count // (4 * size)
    me = lax.axis_index(AXES)
    plane, place = me // width, me % width
    xor = width & (width - 1) == 0

    def partner(spot, step):
        return spot ^ step if xor else (spot + step) % width

    def along(x, step):
        return lax.ppermute(x, AXES, [(i, (i + step * width) % size) for i in range(size)])

    def across(x, step, back):
        pairs = [(i, i // width * width + partner(i % width, step)) for i in range(size)]
        return lax.ppermute(x, AXES, [p[::-1] for p in pairs] if back else pairs)

    experts = jnp.arange(size, dtype=jnp.int32)
    experts = experts // width * width + partner(place, experts % width)
    match = expert_ids.T[None, :, :] == experts[:, None, None]
    named = jnp.any(match, axis=1)
    score = jnp.sum(jnp.where(match, gate_scores.T[None, :, :], 0.0), axis=1)
    earlier = jnp.triu(jnp.ones((token_count, token_count), BF16), 1)
    rank = jnp.dot(named.astype(BF16), earlier, preferred_element_type=F32)
    rank = jnp.where(named, rank, -1.0)
    table = jnp.stack([rank.reshape(planes, width, -1), score.reshape(planes, width, -1)], axis=1)
    table = table.reshape(planes, 2 * width, token_count)

    def facts_of(target):
        return lax.dynamic_index_in_dim(table, target, 0, keepdims=False)

    blocks, facts = [tokens], [facts_of(plane)]
    for s in range(1, planes):
        facts.append(along(facts_of((plane + s) % planes), s))
    for _ in range(1, planes):
        blocks.append(along(blocks[-1], 1))

    outputs = []
    for s in range(planes):
        rows = pack(facts[s], blocks[s], capacity)
        rows = [rows[0]] + [across(rows[m], m, False) for m in range(1, width)]
        outputs.append(ffn(rows, w_gate, w_up, w_down))
    others = []
    for s in [*range(1, planes), 0]:
        rows = outputs[s]
        rows = [rows[0]] + [across(rows[m], m, True) for m in range(1, width)]
        part = mix(facts[s], rows, others, capacity)
        if s:
            others = [along(part, 1)]
    return part


def solution(mesh):
    split = P(AXES, None)
    whole = P(AXES, None, None)
    planes, size = planes_of(mesh), mesh.devices.size

    def step(*arrays):
        return layer(planes, size, *arrays)

    return jax.shard_map(
        step,
        mesh=mesh,
        in_specs=(split, split, split, whole, whole, whole),
        out_specs=split,
        check_vma=False,
    )
```

time: 576 us -> 388 us (0.67)
  blocking collectives: 236 us -> 0 us
  Pallas kernels: 0 us -> 93.7 us
  starting transfers between devices: 4.08 us -> 65 us
  local copies, waits for them, and re-layouts: 48.8 us -> 5.77 us
  matrix products: 32.7 us -> 0.13 us
  other arithmetic: 22.8 us -> 1.64 us
  waiting for transfers between devices: 232 us -> 221 us
    all_to_all x1 -> x0, blocking collectives: 236 us -> none  [per_device(): lax.all_to_all(packed.reshape(experts, capacity, features), ('node', 'loc...]
    all_to_all x1 -> x0, waiting for transfers between devices: 232 us -> none  [per_device(): lax.all_to_all(output.reshape(in_shape), ('node', 'local'), split_axis=0,...]
    ppermute x0 -> x65, waiting for transfers between devices: none -> 221 us  [the longest x56 185 us: across(): return lax.ppermute(x, AXES, [p[::-1] for p in pairs] if back else pairs)]
    pallas_call x0 -> x12, Pallas kernels: none -> 93.7 us  [the longest x4 57.6 us: ffn(): pl.pallas_call(functools.partial(ffn_kernel, pieces, capacity), grid=(ste...]
    ppermute x0 -> x65, starting transfers between devices: none -> 65 us  [the longest x56 54.1 us: across(): return lax.ppermute(x, AXES, [p[::-1] for p in pairs] if back else pairs)]
    dot_general x3 -> x1, matrix products: 32.7 us -> 0.13 us  [layer(): rank = jnp.dot(named.astype(BF16), earlier, preferred_element_type=F32)]
    gather x2 -> x0, local copies, waits for them, and re-layouts: 28.3 us -> none  [the longest x1 20.5 us: per_device(): picked = returned_rows[slot_index].astype(jnp.float32)]
    scatter x1 -> x0, local copies, waits for them, and re-layouts: 18.8 us -> none  [per_device(): jnp.zeros((experts * capacity, features), jnp.bfloat16).at[slot_index]]
  transfers between devices with their start and end apart: 1 -> 65, of which waited for: 1 -> 26; matrix products, arithmetic and copies ran while one was open for 0% -> 1% of each run, Pallas kernels for 0% -> 22%
where the time goes in v1:
time: 388 us; the launch traced here: 387 us
  waiting for transfers between devices  221 us (57%)
  Pallas kernels  93.7 us (24%)
  starting transfers between devices  65 us (17%)
  local copies, waits for them, and re-layouts  5.77 us (1%)
    ppermute x56, waiting for transfers between devices, across(): return lax.ppermute(x, AXES, [p[::-1] for p in pairs] if back else pairs)  185 us
    pallas_call x4, Pallas kernels, ffn(): pl.pallas_call(functools.partial(ffn_kernel, pieces, capacity), grid=(ste...  57.6 us
    ppermute x56, starting transfers between devices, across(): return lax.ppermute(x, AXES, [p[::-1] for p in pairs] if back else pairs)  54.1 us
    ppermute x9, waiting for transfers between devices, along(): lax.ppermute(x, AXES, [(i, (i + step * width) % size) for i in range(size)])  35.5 us
    pallas_call x4, Pallas kernels, mix(): pl.pallas_call(functools.partial(mix_kernel, capacity, experts), grid=(CO...  19.5 us
    pallas_call x4, Pallas kernels, pack(): pl.pallas_call(functools.partial(pack_kernel, capacity), grid=(COLUMN_STE...  16.6 us
    ppermute x9, starting transfers between devices, along(): lax.ppermute(x, AXES, [(i, (i + step * width) % size) for i in range(size)])  10.9 us
  transfers between devices with their start and end apart: 65, of which 26 were waited for; matrix products, arithmetic and copies ran while one was open for 1% of the time, Pallas kernels for 22%

profile of v1, /device:TPU:0, one launch (start us, length us, event | category | flops | bytes accessed | tf_op | source)
XLA Modules:
  0.0 387.2 jit_solution(14297247531663875950)
XLA Ops:
  7.0 21.6 %collective-permute-done.47.facts_ref = f32[16,128]{1,0:T(8,128)S(1)} collective-permute-done((f32[16,128]{1,0:T(8,128)S(1)}, f32[16,128]{1,0:T(8,128)S(1)}, u32[]{:S(2)}, u32[]{:S(2)}) %collective-permute-start.47) | collective-permute-done | bytes 8224 | tf_op jit(solution)/shard_map/ppermute | solution.py:179
  30.2 4.2 %shard_map.70 = (bf16[40,4096]{1,0:T(8,128)(2,1)}, bf16[40,4096]{1,0:T(8,128)(2,1)}, bf16[40,4096]{1,0:T(8,128)(2,1)}, bf16[40,4096]{1,0:T(8,128)(2,1)}, bf16[40...) custom-call(f32[16,128]{1,0:T(8,128)} %copy-done.33, ...), custom_call_target="tpu_custom_call" | custom-call | flops 335544320 | bytes 3670016 | tf_op jit(solution)/shard_map/pallas_call | solution.py:47
  40.4 4.8 %collective-permute-done.49.refs_2_ = bf16[40,4096]{1,0:T(8,128)(2,1)S(1)} collective-permute-done((bf16[40,4096]{1,0:T(8,128)(2,1)}, bf16[40,4096]{1,0:T(8,128)(2,1)S(1)}, u32[]{:S(2)}, u32[]{:S(2)}) %collective-permute-start.49) | collective-permute-done | bytes 327712 | tf_op jit(solution)/shard_map/ppermute | solution.py:183
  46.4 5.0 %collective-permute-done.50.refs_3_ = bf16[40,4096]{1,0:T(8,128)(2,1)S(1)} collective-permute-done((bf16[40,4096]{1,0:T(8,128)(2,1)}, bf16[40,4096]{1,0:T(8,128)(2,1)S(1)}, u32[]{:S(2)}, u32[]{:S(2)}) %collective-permute-start.50) | collective-permute-done | bytes 327712 | tf_op jit(solution)/shard_map/ppermute | solution.py:183
  53.7 13.2 %collective-permute-done.52.refs_5_ = bf16[40,4096]{1,0:T(8,128)(2,1)S(1)} collective-permute-done((bf16[40,4096]{1,0:T(8,128)(2,1)}, bf16[40,4096]{1,0:T(8,128)(2,1)S(1)}, u32[]{:S(2)}, u32[]{:S(2)}) %collective-permute-start.52) | collective-permute-done | bytes 327712 | tf_op jit(solution)/shard_map/ppermute | solution.py:183
  67.9 14.4 %shard_map.71 = (bf16[40,4096]{1,0:T(8,128)(2,1)}, bf16[40,4096]{1,0:T(8,128)(2,1)}, bf16[40,4096]{1,0:T(8,128)(2,1)}, bf16[40,4096]{1,0:T(8,128)(2,1)}, bf16[40...) custom-call(bf16[1,4096,768]{2,1,0:T(8,128)(2,1)} %gate_ref.7, ...), custom_call_target="tpu_custom_call" | custom-call | flops 6039797760 | bytes 24117248 | tf_op jit(solution)/shard_map/pallas_call | solution.py:142
  87.1 4.1 %shard_map.68 = (bf16[40,4096]{1,0:T(8,128)(2,1)}, bf16[40,4096]{1,0:T(8,128)(2,1)}, bf16[40,4096]{1,0:T(8,128)(2,1)}, bf16[40,4096]{1,0:T(8,128)(2,1)}, bf16[40...) custom-call(f32[16,128]{1,0:T(8,128)} %copy-done.31, ...), custom_call_target="tpu_custom_call" | custom-call | flops 335544320 | bytes 3670016 | tf_op jit(solution)/shard_map/pallas_call | solution.py:47
  94.2 5.8 %collective-permute-done.57.refs_3_ = bf16[40,4096]{1,0:T(8,128)(2,1)S(1)} collective-permute-done((bf16[40,4096]{1,0:T(8,128)(2,1)}, bf16[40,4096]{1,0:T(8,128)(2,1)S(1)}, u32[]{:S(2)}, u32[]{:S(2)}) %collective-permute-start.57) | collective-permute-done | bytes 327712 | tf_op jit(solution)/shard_map/ppermute | solution.py:183
  102.4 13.0 %collective-permute-done.59.refs_5_ = bf16[40,4096]{1,0:T(8,128)(2,1)S(1)} collective-permute-done((bf16[40,4096]{1,0:T(8,128)(2,1)}, bf16[40,4096]{1,0:T(8,128)(2,1)S(1)}, u32[]{:S(2)}, u32[]{:S(2)}) %collective-permute-start.59) | collective-permute-done | bytes 327712 | tf_op jit(solution)/shard_map/ppermute | solution.py:183
  122.5 4.7 %shard_map.72 = bf16[128,4096]{1,0:T(8,128)(2,1)} custom-call(f32[16,128]{1,0:T(8,128)} %copy-done.33, bf16[40,4096]{1,0:T(8,128)(2,1)} %get-tuple-element.125.refs_0_, bf16[40,4096]{1,0:T(8,128)(2,1)} %copy-done.24, bf16[40,4096]{1,0:T(8,128)(2,1)} %copy-done.25, bf16[40,4096]{1,0:T(8,128)(2,1)} %copy-done.26, bf16[40,4096]{1,0:T(8,128)(2,1)} %copy-done.27, ...), custom_call_target="tpu_custom_call" | custom-call | flops 671088640 | bytes 4718592 | tf_op jit(solution)/shard_map/pallas_call | solution.py:88
  129.4 18.1 %collective-permute-done.37.refs_5_ = bf16[40,4096]{1,0:T(8,128)(2,1)} collective-permute-done((bf16[40,4096]{1,0:T(8,128)(2,1)}, bf16[40,4096]{1,0:T(8,128)(2,1)}, u32[]{:S(2)}, u32[]{:S(2)}) %collective-permute-start.37) | collective-permute-done | bytes 327712 | tf_op jit(solution)/shard_map/ppermute | solution.py:183
  147.5 14.4 %shard_map.69 = (bf16[40,4096]{1,0:T(8,128)(2,1)}, bf16[40,4096]{1,0:T(8,128)(2,1)}, bf16[40,4096]{1,0:T(8,128)(2,1)}, bf16[40,4096]{1,0:T(8,128)(2,1)}, bf16[40...) custom-call(bf16[1,4096,768]{2,1,0:T(8,128)(2,1)} %gate_ref.7, ...), custom_call_target="tpu_custom_call" | custom-call | flops 6039797760 | bytes 24117248 | tf_op jit(solution)/shard_map/pallas_call | solution.py:142
  164.9 13.9 %collective-permute-done.14.facts_ref = f32[16,128]{1,0:T(8,128)S(1)} collective-permute-done((f32[16,128]{1,0:T(8,128)S(1)}, f32[16,128]{1,0:T(8,128)S(1)}, u32[]{:S(2)}, u32[]{:S(2)}) %collective-permute-start.14) | collective-permute-done | bytes 8224 | tf_op jit(solution)/shard_map/ppermute | solution.py:179
  180.9 7.3 %collective-permute-done.42.refs_3_ = bf16[40,4096]{1,0:T(8,128)(2,1)S(1)} collective-permute-done((bf16[40,4096]{1,0:T(8,128)(2,1)}, bf16[40,4096]{1,0:T(8,128)(2,1)S(1)}, u32[]{:S(2)}, u32[]{:S(2)}) %collective-permute-start.42) | collective-permute-done | bytes 327712 | tf_op jit(solution)/shard_map/ppermute | solution.py:183
  191.6 4.2 %shard_map.66 = (bf16[40,4096]{1,0:T(8,128)(2,1)}, bf16[40,4096]{1,0:T(8,128)(2,1)}, bf16[40,4096]{1,0:T(8,128)(2,1)}, bf16[40,4096]{1,0:T(8,128)(2,1)}, bf16[40...) custom-call(f32[16,128]{1,0:T(8,128)} %copy-done.32, ...), custom_call_target="tpu_custom_call" | custom-call | flops 335544320 | bytes 3670016 | tf_op jit(solution)/shard_map/pallas_call | solution.py:47
  196.5 13.6 %collective-permute-done.44.refs_5_ = bf16[40,4096]{1,0:T(8,128)(2,1)S(1)} collective-permute-done((bf16[40,4096]{1,0:T(8,128)(2,1)}, bf16[40,4096]{1,0:T(8,128)(2,1)S(1)}, u32[]{:S(2)}, u32[]{:S(2)}) %collective-permute-start.44) | collective-permute-done | bytes 327712 | tf_op jit(solution)/shard_map/ppermute | solution.py:183
  215.8 5.2 %collective-permute-done.19.refs_2_ = bf16[40,4096]{1,0:T(8,128)(2,1)} collective-permute-done((bf16[40,4096]{1,0:T(8,128)(2,1)}, bf16[40,4096]{1,0:T(8,128)(2,1)}, u32[]{:S(2)}, u32[]{:S(2)}) %collective-permute-start.19) | collective-permute-done | bytes 327712 | tf_op jit(solution)/shard_map/ppermute | solution.py:183
  221.1 4.9 %shard_map.73 = bf16[128,4096]{1,0:T(8,128)(2,1)} custom-call(f32[16,128]{1,0:T(8,128)} %copy-done.31, bf16[40,4096]{1,0:T(8,128)(2,1)} %get-tuple-element.109.refs_0_, bf16[40,4096]{1,0:T(8,128)(2,1)} %copy-done.3, bf16[40,4096]{1,0:T(8,128)(2,1)} %copy-done.4, bf16[40,4096]{1,0:T(8,128)(2,1)} %copy-done.5, bf16[40,4096]{1,0:T(8,128)(2,1)} %copy-done.6, ...), custom_call_target="tpu_custom_call" | custom-call | flops 671088640 | bytes 4718592 | tf_op jit(solution)/shard_map/pallas_call | solution.py:88
  232.7 10.2 %collective-permute-done.22.refs_5_ = bf16[40,4096]{1,0:T(8,128)(2,1)} collective-permute-done((bf16[40,4096]{1,0:T(8,128)(2,1)}, bf16[40,4096]{1,0:T(8,128)(2,1)}, u32[]{:S(2)}, u32[]{:S(2)}) %collective-permute-start.22) | collective-permute-done | bytes 327712 | tf_op jit(solution)/shard_map/ppermute | solution.py:183
  244.3 14.4 %shard_map.67 = (bf16[40,4096]{1,0:T(8,128)(2,1)}, bf16[40,4096]{1,0:T(8,128)(2,1)}, bf16[40,4096]{1,0:T(8,128)(2,1)}, bf16[40,4096]{1,0:T(8,128)(2,1)}, bf16[40...) custom-call(bf16[1,4096,768]{2,1,0:T(8,128)(2,1)} %gate_ref.7, ...), custom_call_target="tpu_custom_call" | custom-call | flops 6039797760 | bytes 24117248 | tf_op jit(solution)/shard_map/pallas_call | solution.py:142
  263.9 5.7 %collective-permute-done.26.refs_2_ = bf16[40,4096]{1,0:T(8,128)(2,1)S(1)} collective-permute-done((bf16[40,4096]{1,0:T(8,128)(2,1)}, bf16[40,4096]{1,0:T(8,128)(2,1)S(1)}, u32[]{:S(2)}, u32[]{:S(2)}) %collective-permute-start.26) | collective-permute-done | bytes 327712 | tf_op jit(solution)/shard_map/ppermute | solution.py:183
  269.8 5.7 %collective-permute-done.27.refs_3_ = bf16[40,4096]{1,0:T(8,128)(2,1)S(1)} collective-permute-done((bf16[40,4096]{1,0:T(8,128)(2,1)}, bf16[40,4096]{1,0:T(8,128)(2,1)S(1)}, u32[]{:S(2)}, u32[]{:S(2)}) %collective-permute-start.27) | collective-permute-done | bytes 327712 | tf_op jit(solution)/shard_map/ppermute | solution.py:183
  278.5 13.1 %collective-permute-done.29.refs_5_ = bf16[40,4096]{1,0:T(8,128)(2,1)S(1)} collective-permute-done((bf16[40,4096]{1,0:T(8,128)(2,1)}, bf16[40,4096]{1,0:T(8,128)(2,1)S(1)}, u32[]{:S(2)}, u32[]{:S(2)}) %collective-permute-start.29) | collective-permute-done | bytes 327712 | tf_op jit(solution)/shard_map/ppermute | solution.py:183
  295.3 4.9 %shard_map.74 = bf16[128,4096]{1,0:T(8,128)(2,1)} custom-call(f32[16,128]{1,0:T(8,128)} %copy-done.32, bf16[40,4096]{1,0:T(8,128)(2,1)} %get-tuple-element.93.refs_0_, bf16[40,4096]{1,0:T(8,128)(2,1)} %copy-done.8, bf16[40,4096]{1,0:T(8,128)(2,1)} %copy-done.9, bf16[40,4096]{1,0:T(8,128)(2,1)} %copy-done.11, bf16[40,4096]{1,0:T(8,128)(2,1)} %copy-done.13, ...), custom_call_target="tpu_custom_call" | custom-call | flops 671088640 | bytes 4718592 | tf_op jit(solution)/shard_map/pallas_call | solution.py:88
  300.8 12.9 %collective-permute-done.3.refs_4_ = bf16[40,4096]{1,0:T(8,128)(2,1)} collective-permute-done((bf16[40,4096]{1,0:T(8,128)(2,1)}, bf16[40,4096]{1,0:T(8,128)(2,1)}, u32[]{:S(2)}, u32[]{:S(2)}) %collective-permute-start.3) | collective-permute-done | bytes 327712 | tf_op jit(solution)/shard_map/ppermute | solution.py:183
  313.6 5.8 %collective-permute-done.4.refs_5_ = bf16[40,4096]{1,0:T(8,128)(2,1)} collective-permute-done((bf16[40,4096]{1,0:T(8,128)(2,1)}, bf16[40,4096]{1,0:T(8,128)(2,1)}, u32[]{:S(2)}, u32[]{:S(2)}) %collective-permute-start.4) | collective-permute-done | bytes 327712 | tf_op jit(solution)/shard_map/ppermute | solution.py:183
  319.5 14.4 %shard_map.65 = (bf16[40,4096]{1,0:T(8,128)(2,1)}, bf16[40,4096]{1,0:T(8,128)(2,1)}, bf16[40,4096]{1,0:T(8,128)(2,1)}, bf16[40,4096]{1,0:T(8,128)(2,1)}, bf16[40...) custom-call(bf16[1,4096,768]{2,1,0:T(8,128)(2,1)} %gate_ref.7, ...), custom_call_target="tpu_custom_call" | custom-call | flops 6039797760 | bytes 24117248 | tf_op jit(solution)/shard_map/pallas_call | solution.py:142
  338.3 20.4 %collective-permute-done.10.refs_4_ = bf16[40,4096]{1,0:T(8,128)(2,1)S(1)} collective-permute-done((bf16[40,4096]{1,0:T(8,128)(2,1)}, bf16[40,4096]{1,0:T(8,128)(2,1)S(1)}, u32[]{:S(2)}, u32[]{:S(2)}) %collective-permute-start.10) | collective-permute-done | bytes 327712 | tf_op jit(solution)/shard_map/ppermute | solution.py:183
  358.7 6.3 %collective-permute-done.11.refs_5_ = bf16[40,4096]{1,0:T(8,128)(2,1)S(1)} collective-permute-done((bf16[40,4096]{1,0:T(8,128)(2,1)}, bf16[40,4096]{1,0:T(8,128)(2,1)S(1)}, u32[]{:S(2)}, u32[]{:S(2)}) %collective-permute-start.11) | collective-permute-done | bytes 327712 | tf_op jit(solution)/shard_map/ppermute | solution.py:183
  366.6 9.2 %collective-permute-done.8.refs_2_ = bf16[40,4096]{1,0:T(8,128)(2,1)S(1)} collective-permute-done((bf16[40,4096]{1,0:T(8,128)(2,1)}, bf16[40,4096]{1,0:T(8,128)(2,1)S(1)}, u32[]{:S(2)}, u32[]{:S(2)}) %collective-permute-start.8) | collective-permute-done | bytes 327712 | tf_op jit(solution)/shard_map/ppermute | solution.py:183
  375.8 5.4 %collective-permute-done.9.refs_3_ = bf16[40,4096]{1,0:T(8,128)(2,1)S(1)} collective-permute-done((bf16[40,4096]{1,0:T(8,128)(2,1)}, bf16[40,4096]{1,0:T(8,128)(2,1)S(1)}, u32[]{:S(2)}, u32[]{:S(2)}) %collective-permute-start.9) | collective-permute-done | bytes 327712 | tf_op jit(solution)/shard_map/ppermute | solution.py:183
  382.3 4.9 %shard_map.75 = bf16[128,4096]{1,0:T(8,128)(2,1)} custom-call(f32[16,128]{1,0:T(8,128)} %get-tuple-element.136.facts_ref, bf16[40,4096]{1,0:T(8,128)(2,1)} %get-tuple-element.77.refs_0_, bf16[40,4096]{1,0:T(8,128)(2,1)} %copy-done.21, bf16[40,4096]{1,0:T(8,128)(2,1)} %copy-done.22, bf16[40,4096]{1,0:T(8,128)(2,1)} %copy-done.23, ...), custom_call_target="tpu_custom_call" | custom-call | flops 671088640 | bytes 4718592 | tf_op jit(solution)/shard_map/pallas_call | solution.py:88
  (214 shorter events, 80.8 us)
Async XLA Ops:
  0.0 28.6 %collective-permute-start.15 = (bf16[128,4096]{1,0:T(8,128)(2,1)}, bf16[128,4096]{1,0:T(8,128)(2,1)S(1)}, u32[]{:S(2)}, u32[]{:S(2)}) collective-permute-start(bf16[128,4096]{1,0:T(8,128)(2,1)} %rows_ref.1), channel_id=1, source_target_pairs={{0,8},{1,9},{2,10},{3,11},{4,12},{5,13},{6,14},{7,15},{8,16},{9,17... | collective-permute-start | bytes 3145736 | tf_op jit(solution)/shard_map/ppermute | solution.py:179
  37.8 29.1 %collective-permute-start.52 = (bf16[40,4096]{1,0:T(8,128)(2,1)}, bf16[40,4096]{1,0:T(8,128)(2,1)S(1)}, u32[]{:S(2)}, u32[]{:S(2)}) collective-permute-start(bf16[40,4096]{1,0:T(8,128)(2,1)} %get-tuple-element.122), channel_id=1, source_target_pairs={{0,5},{1,4},{2,7},{3,6},{4,1},{5,0},{6,3},{7,2},{8,13},{9,12},{10,... | collective-permute-start | bytes 983048 | tf_op jit(solution)/shard_map/ppermute | solution.py:183
  38.0 28.9 %collective-permute-start.53 = (bf16[40,4096]{1,0:T(8,128)(2,1)}, bf16[40,4096]{1,0:T(8,128)(2,1)S(1)}, u32[]{:S(2)}, u32[]{:S(2)}) collective-permute-start(bf16[40,4096]{1,0:T(8,128)(2,1)} %get-tuple-element.123), channel_id=1, source_target_pairs={{0,6},{1,7},{2,4},{3,5},{4,2},{5,3},{6,0},{7,1},{8,14},{9,15},{10,... | collective-permute-start | bytes 983048 | tf_op jit(solution)/shard_map/ppermute | solution.py:183
  51.4 34.7 %collective-permute-start.16 = (bf16[128,4096]{1,0:T(8,128)(2,1)}, bf16[128,4096]{1,0:T(8,128)(2,1)S(1)}, u32[]{:S(2)}, u32[]{:S(2)}) collective-permute-start(bf16[128,4096]{1,0:T(8,128)(2,1)} %copy-done.34), channel_id=1, source_target_pairs={{0,8},{1,9},{2,10},{3,11},{4,12},{5,13},{6,14},{7,15},{8,16},{9,17... | collective-permute-start | bytes 3145736 | tf_op jit(solution)/shard_map/ppermute | solution.py:179
  51.4 33.1 %collective-permute-start.32 = (f32[16,128]{1,0:T(8,128)S(1)}, f32[16,128]{1,0:T(8,128)S(1)}, u32[]{:S(2)}, u32[]{:S(2)}) collective-permute-start(f32[16,128]{1,0:T(8,128)S(1)} %get-tuple-element.134), channel_id=1, source_target_pairs={{0,16},{1,17},{2,18},{3,19},{4,20},{5,21},{6,22},{7,23},{8,24},{9,... | collective-permute-start | bytes 24584 | tf_op jit(solution)/shard_map/ppermute | solution.py:179
  86.1 29.3 %collective-permute-start.59 = (bf16[40,4096]{1,0:T(8,128)(2,1)}, bf16[40,4096]{1,0:T(8,128)(2,1)S(1)}, u32[]{:S(2)}, u32[]{:S(2)}) collective-permute-start(bf16[40,4096]{1,0:T(8,128)(2,1)} %get-tuple-element.130), channel_id=1, source_target_pairs={{5,0},{4,1},{7,2},{6,3},{1,4},{0,5},{3,6},{2,7},{13,8},{12,9},{15,... | collective-permute-start | bytes 983048 | tf_op jit(solution)/shard_map/ppermute | solution.py:183
  91.2 26.0 %collective-permute-start.60 = (bf16[40,4096]{1,0:T(8,128)(2,1)}, bf16[40,4096]{1,0:T(8,128)(2,1)S(1)}, u32[]{:S(2)}, u32[]{:S(2)}) collective-permute-start(bf16[40,4096]{1,0:T(8,128)(2,1)} %get-tuple-element.131), channel_id=1, source_target_pairs={{6,0},{7,1},{4,2},{5,3},{2,4},{3,5},{0,6},{1,7},{14,8},{15,9},{12,... | collective-permute-start | bytes 983048 | tf_op jit(solution)/shard_map/ppermute | solution.py:183
  93.8 25.0 %collective-permute-start.61 = (bf16[40,4096]{1,0:T(8,128)(2,1)}, bf16[40,4096]{1,0:T(8,128)(2,1)S(1)}, u32[]{:S(2)}, u32[]{:S(2)}) collective-permute-start(bf16[40,4096]{1,0:T(8,128)(2,1)} %get-tuple-element.132), channel_id=1, source_target_pairs={{7,0},{6,1},{5,2},{4,3},{3,4},{2,5},{1,6},{0,7},{15,8},{14,9},{13,... | collective-permute-start | bytes 983048 | tf_op jit(solution)/shard_map/ppermute | solution.py:183
  118.8 28.6 %collective-permute-start.37 = (bf16[40,4096]{1,0:T(8,128)(2,1)}, bf16[40,4096]{1,0:T(8,128)(2,1)}, u32[]{:S(2)}, u32[]{:S(2)}) collective-permute-start(bf16[40,4096]{1,0:T(8,128)(2,1)} %get-tuple-element.106), channel_id=1, source_target_pairs={{0,5},{1,4},{2,7},{3,6},{4,1},{5,0},{6,3},{7,2},{8,13},{9,12},{10,... | collective-permute-start | bytes 983048 | tf_op jit(solution)/shard_map/ppermute | solution.py:183
  118.8 28.6 %collective-permute-start.38 = (bf16[40,4096]{1,0:T(8,128)(2,1)}, bf16[40,4096]{1,0:T(8,128)(2,1)}, u32[]{:S(2)}, u32[]{:S(2)}) collective-permute-start(bf16[40,4096]{1,0:T(8,128)(2,1)} %get-tuple-element.107), channel_id=1, source_target_pairs={{0,6},{1,7},{2,4},{3,5},{4,2},{5,3},{6,0},{7,1},{8,14},{9,15},{10,... | collective-permute-start | bytes 983048 | tf_op jit(solution)/shard_map/ppermute | solution.py:183
  121.9 25.5 %collective-permute-start.39 = (bf16[40,4096]{1,0:T(8,128)(2,1)}, bf16[40,4096]{1,0:T(8,128)(2,1)}, u32[]{:S(2)}, u32[]{:S(2)}) collective-permute-start(bf16[40,4096]{1,0:T(8,128)(2,1)} %get-tuple-element.108), channel_id=1, source_target_pairs={{0,7},{1,6},{2,5},{3,4},{4,3},{5,2},{6,1},{7,0},{8,15},{9,14},{10,... | collective-permute-start | bytes 983048 | tf_op jit(solution)/shard_map/ppermute | solution.py:183
  128.1 85.1 %collective-permute-start.62 = (bf16[128,4096]{1,0:T(8,128)(2,1)}, bf16[128,4096]{1,0:T(8,128)(2,1)S(1)}, u32[]{:S(2)}, u32[]{:S(2)}) collective-permute-start(bf16[128,4096]{1,0:T(8,128)(2,1)} %shard_map.72), channel_id=1, source_target_pairs={{0,8},{1,9},{2,10},{3,11},{4,12},{5,13},{6,14},{7,15},{8,16},{9,17... | collective-permute-start | bytes 3145736 | tf_op jit(solution)/shard_map/ppermute | solution.py:179
  128.2 62.4 %collective-permute-start.17 = (bf16[128,4096]{1,0:T(8,128)(2,1)}, bf16[128,4096]{1,0:T(8,128)(2,1)S(1)}, u32[]{:S(2)}, u32[]{:S(2)}) collective-permute-start(bf16[128,4096]{1,0:T(8,128)(2,1)} %copy-done.35), channel_id=1, source_target_pairs={{0,8},{1,9},{2,10},{3,11},{4,12},{5,13},{6,14},{7,15},{8,16},{9,17... | collective-permute-start | bytes 3145736 | tf_op jit(solution)/shard_map/ppermute | solution.py:179
  180.4 29.7 %collective-permute-start.44 = (bf16[40,4096]{1,0:T(8,128)(2,1)}, bf16[40,4096]{1,0:T(8,128)(2,1)S(1)}, u32[]{:S(2)}, u32[]{:S(2)}) collective-permute-start(bf16[40,4096]{1,0:T(8,128)(2,1)} %get-tuple-element.114), channel_id=1, source_target_pairs={{5,0},{4,1},{7,2},{6,3},{1,4},{0,5},{3,6},{2,7},{13,8},{12,9},{15,... | collective-permute-start | bytes 983048 | tf_op jit(solution)/shard_map/ppermute | solution.py:183
  213.2 29.8 %collective-permute-start.22 = (bf16[40,4096]{1,0:T(8,128)(2,1)}, bf16[40,4096]{1,0:T(8,128)(2,1)}, u32[]{:S(2)}, u32[]{:S(2)}) collective-permute-start(bf16[40,4096]{1,0:T(8,128)(2,1)} %get-tuple-element.90), channel_id=1, source_target_pairs={{0,5},{1,4},{2,7},{3,6},{4,1},{5,0},{6,3},{7,2},{8,13},{9,12},{10,... | collective-permute-start | bytes 983048 | tf_op jit(solution)/shard_map/ppermute | solution.py:183
  213.6 30.7 %collective-permute-start.23 = (bf16[40,4096]{1,0:T(8,128)(2,1)}, bf16[40,4096]{1,0:T(8,128)(2,1)}, u32[]{:S(2)}, u32[]{:S(2)}) collective-permute-start(bf16[40,4096]{1,0:T(8,128)(2,1)} %get-tuple-element.91), channel_id=1, source_target_pairs={{0,6},{1,7},{2,4},{3,5},{4,2},{5,3},{6,0},{7,1},{8,14},{9,15},{10,... | collective-permute-start | bytes 983048 | tf_op jit(solution)/shard_map/ppermute | solution.py:183
  221.0 23.3 %collective-permute-start.24 = (bf16[40,4096]{1,0:T(8,128)(2,1)}, bf16[40,4096]{1,0:T(8,128)(2,1)}, u32[]{:S(2)}, u32[]{:S(2)}) collective-permute-start(bf16[40,4096]{1,0:T(8,128)(2,1)} %get-tuple-element.92), channel_id=1, source_target_pairs={{0,7},{1,6},{2,5},{3,4},{4,3},{5,2},{6,1},{7,0},{8,15},{9,14},{10,... | collective-permute-start | bytes 983048 | tf_op jit(solution)/shard_map/ppermute | solution.py:183
  226.8 35.3 %collective-permute-start.63 = (bf16[128,4096]{1,0:T(8,128)(2,1)}, bf16[128,4096]{1,0:T(8,128)(2,1)S(1)}, u32[]{:S(2)}, u32[]{:S(2)}) collective-permute-start(bf16[128,4096]{1,0:T(8,128)(2,1)} %shard_map.73), channel_id=1, source_target_pairs={{0,8},{1,9},{2,10},{3,11},{4,12},{5,13},{6,14},{7,15},{8,16},{9,17... | collective-permute-start | bytes 3145736 | tf_op jit(solution)/shard_map/ppermute | solution.py:179
  231.4 28.1 %collective-permute-start = (bf16[40,4096]{1,0:T(8,128)(2,1)}, bf16[40,4096]{1,0:T(8,128)(2,1)S(1)}, u32[]{:S(2)}, u32[]{:S(2)}) collective-permute-start(bf16[40,4096]{1,0:T(8,128)(2,1)} %get-tuple-element.70), channel_id=1, source_target_pairs={{0,1},{1,0},{2,3},{3,2},{4,5},{5,4},{6,7},{7,6},{8,9},{9,8},{10,11... | collective-permute-start | bytes 983048 | tf_op jit(solution)/shard_map/ppermute | solution.py:183
  262.1 29.5 %collective-permute-start.29 = (bf16[40,4096]{1,0:T(8,128)(2,1)}, bf16[40,4096]{1,0:T(8,128)(2,1)S(1)}, u32[]{:S(2)}, u32[]{:S(2)}) collective-permute-start(bf16[40,4096]{1,0:T(8,128)(2,1)} %get-tuple-element.98), channel_id=1, source_target_pairs={{5,0},{4,1},{7,2},{6,3},{1,4},{0,5},{3,6},{2,7},{13,8},{12,9},{15,... | collective-permute-start | bytes 983048 | tf_op jit(solution)/shard_map/ppermute | solution.py:183
  262.3 31.5 %collective-permute-start.30 = (bf16[40,4096]{1,0:T(8,128)(2,1)}, bf16[40,4096]{1,0:T(8,128)(2,1)S(1)}, u32[]{:S(2)}, u32[]{:S(2)}) collective-permute-start(bf16[40,4096]{1,0:T(8,128)(2,1)} %get-tuple-element.99), channel_id=1, source_target_pairs={{6,0},{7,1},{4,2},{5,3},{2,4},{3,5},{0,6},{1,7},{14,8},{15,9},{12,... | collective-permute-start | bytes 983048 | tf_op jit(solution)/shard_map/ppermute | solution.py:183
  269.6 24.8 %collective-permute-start.31 = (bf16[40,4096]{1,0:T(8,128)(2,1)}, bf16[40,4096]{1,0:T(8,128)(2,1)S(1)}, u32[]{:S(2)}, u32[]{:S(2)}) collective-permute-start(bf16[40,4096]{1,0:T(8,128)(2,1)} %get-tuple-element.100), channel_id=1, source_target_pairs={{7,0},{6,1},{5,2},{4,3},{3,4},{2,5},{1,6},{0,7},{15,8},{14,9},{13,... | collective-permute-start | bytes 983048 | tf_op jit(solution)/shard_map/ppermute | solution.py:183
  275.6 24.7 %collective-permute-start.2 = (bf16[40,4096]{1,0:T(8,128)(2,1)}, bf16[40,4096]{1,0:T(8,128)(2,1)}, u32[]{:S(2)}, u32[]{:S(2)}) collective-permute-start(bf16[40,4096]{1,0:T(8,128)(2,1)} %get-tuple-element.72), channel_id=1, source_target_pairs={{0,3},{1,2},{2,1},{3,0},{4,7},{5,6},{6,5},{7,4},{8,11},{9,10},{10,... | collective-permute-start | bytes 983048 | tf_op jit(solution)/shard_map/ppermute | solution.py:183
  277.0 36.7 %collective-permute-start.3 = (bf16[40,4096]{1,0:T(8,128)(2,1)}, bf16[40,4096]{1,0:T(8,128)(2,1)}, u32[]{:S(2)}, u32[]{:S(2)}) collective-permute-start(bf16[40,4096]{1,0:T(8,128)(2,1)} %get-tuple-element.73), channel_id=1, source_target_pairs={{0,4},{1,5},{2,6},{3,7},{4,0},{5,1},{6,2},{7,3},{8,12},{9,13},{10,... | collective-permute-start | bytes 983048 | tf_op jit(solution)/shard_map/ppermute | solution.py:183
  291.6 27.8 %collective-permute-start.4 = (bf16[40,4096]{1,0:T(8,128)(2,1)}, bf16[40,4096]{1,0:T(8,128)(2,1)}, u32[]{:S(2)}, u32[]{:S(2)}) collective-permute-start(bf16[40,4096]{1,0:T(8,128)(2,1)} %get-tuple-element.74), channel_id=1, source_target_pairs={{0,5},{1,4},{2,7},{3,6},{4,1},{5,0},{6,3},{7,2},{8,13},{9,12},{10,... | collective-permute-start | bytes 983048 | tf_op jit(solution)/shard_map/ppermute | solution.py:183
  293.8 25.6 %collective-permute-start.5 = (bf16[40,4096]{1,0:T(8,128)(2,1)}, bf16[40,4096]{1,0:T(8,128)(2,1)}, u32[]{:S(2)}, u32[]{:S(2)}) collective-permute-start(bf16[40,4096]{1,0:T(8,128)(2,1)} %get-tuple-element.75), channel_id=1, source_target_pairs={{0,6},{1,7},{2,4},{3,5},{4,2},{5,3},{6,0},{7,1},{8,14},{9,15},{10,... | collective-permute-start | bytes 983048 | tf_op jit(solution)/shard_map/ppermute | solution.py:183
  294.4 25.0 %collective-permute-start.6 = (bf16[40,4096]{1,0:T(8,128)(2,1)}, bf16[40,4096]{1,0:T(8,128)(2,1)}, u32[]{:S(2)}, u32[]{:S(2)}) collective-permute-start(bf16[40,4096]{1,0:T(8,128)(2,1)} %get-tuple-element.76), channel_id=1, source_target_pairs={{0,7},{1,6},{2,5},{3,4},{4,3},{5,2},{6,1},{7,0},{8,15},{9,14},{10,... | collective-permute-start | bytes 983048 | tf_op jit(solution)/shard_map/ppermute | solution.py:183
  300.2 81.0 %collective-permute-start.64 = (bf16[128,4096]{1,0:T(8,128)(2,1)}, bf16[128,4096]{1,0:T(8,128)(2,1)S(1)}, u32[]{:S(2)}, u32[]{:S(2)}) collective-permute-start(bf16[128,4096]{1,0:T(8,128)(2,1)} %shard_map.74), channel_id=1, source_target_pairs={{0,8},{1,9},{2,10},{3,11},{4,12},{5,13},{6,14},{7,15},{8,16},{9,17... | collective-permute-start | bytes 3145736 | tf_op jit(solution)/shard_map/ppermute | solution.py:179
  333.9 24.8 %collective-permute-start.10 = (bf16[40,4096]{1,0:T(8,128)(2,1)}, bf16[40,4096]{1,0:T(8,128)(2,1)S(1)}, u32[]{:S(2)}, u32[]{:S(2)}) collective-permute-start(bf16[40,4096]{1,0:T(8,128)(2,1)} %get-tuple-element.81), channel_id=1, source_target_pairs={{4,0},{5,1},{6,2},{7,3},{0,4},{1,5},{2,6},{3,7},{12,8},{13,9},{14,... | collective-permute-start | bytes 983048 | tf_op jit(solution)/shard_map/ppermute | solution.py:183
  335.4 29.7 %collective-permute-start.11 = (bf16[40,4096]{1,0:T(8,128)(2,1)}, bf16[40,4096]{1,0:T(8,128)(2,1)S(1)}, u32[]{:S(2)}, u32[]{:S(2)}) collective-permute-start(bf16[40,4096]{1,0:T(8,128)(2,1)} %get-tuple-element.82), channel_id=1, source_target_pairs={{5,0},{4,1},{7,2},{6,3},{1,4},{0,5},{3,6},{2,7},{13,8},{12,9},{15,... | collective-permute-start | bytes 983048 | tf_op jit(solution)/shard_map/ppermute | solution.py:183
  335.8 29.8 %collective-permute-start.12 = (bf16[40,4096]{1,0:T(8,128)(2,1)}, bf16[40,4096]{1,0:T(8,128)(2,1)S(1)}, u32[]{:S(2)}, u32[]{:S(2)}) collective-permute-start(bf16[40,4096]{1,0:T(8,128)(2,1)} %get-tuple-element.83), channel_id=1, source_target_pairs={{6,0},{7,1},{4,2},{5,3},{2,4},{3,5},{0,6},{1,7},{14,8},{15,9},{12,... | collective-permute-start | bytes 983048 | tf_op jit(solution)/shard_map/ppermute | solution.py:183
  337.4 29.2 %collective-permute-start.13 = (bf16[40,4096]{1,0:T(8,128)(2,1)}, bf16[40,4096]{1,0:T(8,128)(2,1)S(1)}, u32[]{:S(2)}, u32[]{:S(2)}) collective-permute-start(bf16[40,4096]{1,0:T(8,128)(2,1)} %get-tuple-element.84), channel_id=1, source_target_pairs={{7,0},{6,1},{5,2},{4,3},{3,4},{2,5},{1,6},{0,7},{15,8},{14,9},{13,... | collective-permute-start | bytes 983048 | tf_op jit(solution)/shard_map/ppermute | solution.py:183
  (82 other events, 1257.1 us)

commit v2 on v1

--- a/solution.py
+++ b/solution.py
@@ -12,7 +12,8 @@
 AXES = ("node", "local")
 BF16 = jnp.bfloat16
 F32 = jnp.float32
-COLUMN_STEPS = 4
+COLUMN_STEPS = 2
+HALVES = 2
 
 
 def planes_of(mesh):
@@ -23,6 +24,10 @@
     if count > 1 and all(len(set(r.tolist())) == 1 for r in rows):
         return count
     return 1
+
+
+def parts_of(s, planes):
+    return HALVES if 0 < s == planes - 1 else 1
 
 
 def picks(table, capacity):
@@ -61,8 +66,9 @@
     )(facts, rows)
 
 
-def mix_kernel(capacity, experts, facts_ref, *refs):
-    *rows, out_ref = refs
+def mix_kernel(capacity, experts, extra, facts_ref, *refs):
+    out_ref = refs[-1]
+    rows = refs[:experts]
     weight = jnp.concatenate(
         [
             jnp.where(r, facts_ref[experts + e : experts + e + 1, :], 0.0)
@@ -73,34 +79,38 @@
     high = weight.astype(BF16)
     low = (weight - high.astype(F32)).astype(BF16)
     dims = (((0,), (0,)), ((), ()))
-    value = jnp.concatenate([r[...] for r in rows[:experts]], axis=0)
+    value = jnp.concatenate([r[...] for r in rows], axis=0)
     total = lax.dot_general(high, value, dims, preferred_element_type=F32)
     total += lax.dot_general(low, value, dims, preferred_element_type=F32)
-    for other in rows[experts:]:
-        total += other[...].astype(F32)
+    for half, other in enumerate(refs[experts:-1]):
+        if extra == 1:
+            total += other[...].astype(F32)
+        else:
+            total += jnp.where(pl.program_id(0) == half, other[...].astype(F32), 0.0)
     out_ref[...] = total.astype(out_ref.dtype)
 
 
-def mix(facts, rows, others, capacity):
-    experts, count, features = facts.shape[0] // 2, facts.shape[1], rows[0].shape[1]
-    step = features // COLUMN_STEPS
-    tall = [pl.BlockSpec((r.shape[0], step), lambda i: (0, i)) for r in [*rows, *others]]
+def mix(facts, rows, others, capacity, step, first, steps):
+    experts, count = facts.shape[0] // 2, facts.shape[1]
+    specs = [pl.BlockSpec(facts.shape, lambda i: (0, 0))]
+    specs += [pl.BlockSpec((r.shape[0], step), lambda i: (0, first + i)) for r in rows]
+    specs += [pl.BlockSpec((count, step), lambda i: (0, 0)) for _ in others]
     return pl.pallas_call(
-        functools.partial(mix_kernel, capacity, experts),
-        grid=(COLUMN_STEPS,),
-        in_specs=[pl.BlockSpec(facts.shape, lambda i: (0, 0)), *tall],
+        functools.partial(mix_kernel, capacity, experts, len(others)),
+        grid=(steps,),
+        in_specs=specs,
         out_specs=pl.BlockSpec((count, step), lambda i: (0, i)),
-        out_shape=jax.ShapeDtypeStruct((count, features), BF16),
+        out_shape=jax.ShapeDtypeStruct((count, steps * step), BF16),
         cost_estimate=pl.CostEstimate(
-            flops=4 * experts * capacity * count * features,
-            bytes_accessed=2 * (experts * capacity + 2 * count) * features,
+            flops=4 * experts * capacity * count * step * steps,
+            bytes_accessed=2 * (experts * capacity + 2 * count) * step * steps,
             transcendentals=0,
         ),
     )(facts, *rows, *others)
 
 
 def ffn_kernel(pieces, capacity, gate_ref, up_ref, down_ref, *refs):
-    rows, outs, (held, total) = refs[:pieces], refs[pieces : 2 * pieces], refs[2 * pieces :]
+    rows, outs, (held, total) = refs[:pieces], refs[pieces:-2], refs[-2:]
     step, last = pl.program_id(0), pl.num_programs(0) - 1
 
     @pl.when(step == 0)
@@ -128,18 +138,21 @@
 
     @pl.when(step == last)
     def _():
-        for m in range(pieces):
-            outs[m][...] = total[m * capacity : (m + 1) * capacity, :].astype(BF16)
-
-
-def ffn(rows, w_gate, w_up, w_down):
+        for k, out in enumerate(outs):
+            part, m = divmod(k, pieces)
+            columns = slice(part * out.shape[1], (part + 1) * out.shape[1])
+            out[...] = total[m * capacity : (m + 1) * capacity, columns].astype(BF16)
+
+
+def ffn(rows, w_gate, w_up, w_down, parts):
     pieces, (capacity, features) = len(rows), rows[0].shape
     hidden = w_gate.shape[2]
     tile = 256 if hidden % 256 == 0 else hidden
     steps = hidden // tile
     whole = pl.BlockSpec((capacity, features), lambda i: (0, 0))
+    piece = (capacity, features // parts)
     count = pieces * capacity
-    return pl.pallas_call(
+    outs = pl.pallas_call(
         functools.partial(ffn_kernel, pieces, capacity),
         grid=(steps,),
         in_specs=[
@@ -148,8 +161,8 @@
             pl.BlockSpec((1, tile, features), lambda i: (0, i, 0)),
         ]
         + [whole] * pieces,
-        out_specs=[whole] * pieces,
-        out_shape=[jax.ShapeDtypeStruct((capacity, features), BF16)] * pieces,
+        out_specs=[pl.BlockSpec(piece, lambda i: (0, 0))] * (pieces * parts),
+        out_shape=[jax.ShapeDtypeStruct(piece, BF16)] * (pieces * parts),
         scratch_shapes=[
             pltpu.VMEM((count, features), BF16),
             pltpu.VMEM((count, features), F32),
@@ -161,11 +174,12 @@
             transcendentals=count * hidden,
         ),
     )(w_gate, w_up, w_down, *rows)
+    return [outs[k * pieces : (k + 1) * pieces] for k in range(parts)]
 
 
 def layer(planes, size, tokens, expert_ids, gate_scores, w_gate, w_up, w_down):
     width = size // planes
-    token_count, _ = tokens.shape
+    token_count, features = tokens.shape
     top_count = expert_ids.shape[1]
     capacity = 5 * token_count * top_count // (4 * size)
     me = lax.axis_index(AXES)
@@ -206,15 +220,24 @@
     for s in range(planes):
         rows = pack(facts[s], blocks[s], capacity)
         rows = [rows[0]] + [across(rows[m], m, False) for m in range(1, width)]
-        outputs.append(ffn(rows, w_gate, w_up, w_down))
-    others = []
-    for s in [*range(1, planes), 0]:
-        rows = outputs[s]
-        rows = [rows[0]] + [across(rows[m], m, True) for m in range(1, width)]
-        part = mix(facts[s], rows, others, capacity)
-        if s:
-            others = [along(part, 1)]
-    return part
+        outputs.append(ffn(rows, w_gate, w_up, w_down, parts_of(s, planes)))
+
+    def returned(s):
+        return [
+            [rows[0]] + [across(rows[m], m, True) for m in range(1, width)]
+            for rows in outputs[s]
+        ]
+
+    step = features // HALVES
+    others = [[] for _ in range(HALVES)]
+    for s in range(1, planes):
+        parts = returned(s)
+        for half in range(HALVES):
+            rows = parts[half] if len(parts) > 1 else parts[0]
+            first = half if len(parts) == 1 else 0
+            piece = mix(facts[s], rows, others[half], capacity, step, first, 1)
+            others[half] = [along(piece, 1)]
+    return mix(facts[0], returned(0)[0], sum(others, []), capacity, step, 0, HALVES)
 
 
 def solution(mesh):

time: 388 us -> 369 us (0.951)
  waiting for transfers between devices: 221 us -> 190 us
  starting transfers between devices: 65 us -> 75.3 us
    ppermute x56 -> x63, waiting for transfers between devices: 185 us -> 144 us  [across(): return lax.ppermute(x, AXES, [p[::-1] for p in pairs] if back else pairs)]
    ppermute x9 -> x12, waiting for transfers between devices: 35.5 us -> 46 us  [along(): lax.ppermute(x, AXES, [(i, (i + step * width) % size) for i in range(size)])]
    ppermute x56 -> x63, starting transfers between devices: 54.1 us -> 64.4 us  [across(): return lax.ppermute(x, AXES, [p[::-1] for p in pairs] if back else pairs)]
    pallas_call x4, Pallas kernels: 16.6 us -> 12.3 us  [pack(): pl.pallas_call(functools.partial(pack_kernel, capacity), grid=(COLUMN_STE...]
    pallas_call x4 -> x7, Pallas kernels: 19.5 us -> 22.7 us  [mix(): pl.pallas_call(functools.partial(mix_kernel, capacity, experts, len(other...]
    ppermute x9 -> x12, starting transfers between devices: 10.9 us -> 11 us  [along(): lax.ppermute(x, AXES, [(i, (i + step * width) % size) for i in range(size)])]
  transfers between devices with their start and end apart: 65 -> 75, of which waited for: 26 -> 21; matrix products, arithmetic and copies ran while one was open for 1% -> 1% of each run, Pallas kernels for 22% -> 23%
where the time goes in v2:
time: 369 us; the launch traced here: 368 us
  waiting for transfers between devices  190 us (51%)
  Pallas kernels  92.9 us (25%)
  starting transfers between devices  75.3 us (20%)
  local copies, waits for them, and re-layouts  7.39 us (2%)
    ppermute x63, waiting for transfers between devices, across(): return lax.ppermute(x, AXES, [p[::-1] for p in pairs] if back else pairs)  144 us
    ppermute x63, starting transfers between devices, across(): return lax.ppermute(x, AXES, [p[::-1] for p in pairs] if back else pairs)  64.4 us
    pallas_call x4, Pallas kernels, ffn(): pl.pallas_call(functools.partial(ffn_kernel, pieces, capacity), grid=(ste...  58 us
    ppermute x12, waiting for transfers between devices, along(): lax.ppermute(x, AXES, [(i, (i + step * width) % size) for i in range(size)])  46 us
    pallas_call x7, Pallas kernels, mix(): pl.pallas_call(functools.partial(mix_kernel, capacity, experts, len(other...  22.7 us
    pallas_call x4, Pallas kernels, pack(): pl.pallas_call(functools.partial(pack_kernel, capacity), grid=(COLUMN_STE...  12.3 us
    ppermute x12, starting transfers between devices, along(): lax.ppermute(x, AXES, [(i, (i + step * width) % size) for i in range(size)])  11 us
  transfers between devices with their start and end apart: 75, of which 21 were waited for; matrix products, arithmetic and copies ran while one was open for 1% of the time, Pallas kernels for 23%

profile of v2, /device:TPU:0, one launch (start us, length us, event | category | flops | bytes accessed | tf_op | source)
XLA Modules:
  0.0 368.1 jit_solution(15410846682470090135)
XLA Ops:
  0.0 3.1 collective-permute-start.15
  7.0 21.6 %collective-permute-done.47.facts_ref = f32[16,128]{1,0:T(8,128)S(1)} collective-permute-done((f32[16,128]{1,0:T(8,128)S(1)}, f32[16,128]{1,0:T(8,128)S(1)}, u32[]{:S(2)}, u32[]{:S(2)}) %collective-permute-start.47) | collective-permute-done | bytes 8224 | tf_op jit(solution)/shard_map/ppermute | solution.py:193
  30.2 3.0 shard_map.70
  39.2 4.8 %collective-permute-done.49.refs_2_ = bf16[40,4096]{1,0:T(8,128)(2,1)S(1)} collective-permute-done((bf16[40,4096]{1,0:T(8,128)(2,1)}, bf16[40,4096]{1,0:T(8,128)(2,1)S(1)}, u32[]{:S(2)}, u32[]{:S(2)}) %collective-permute-start.49) | collective-permute-done | bytes 327712 | tf_op jit(solution)/shard_map/ppermute | solution.py:197
  45.2 3.0 shard_map.64
  52.7 12.7 %collective-permute-done.52.refs_5_ = bf16[40,4096]{1,0:T(8,128)(2,1)S(1)} collective-permute-done((bf16[40,4096]{1,0:T(8,128)(2,1)}, bf16[40,4096]{1,0:T(8,128)(2,1)S(1)}, u32[]{:S(2)}, u32[]{:S(2)}) %collective-permute-start.52) | collective-permute-done | bytes 327712 | tf_op jit(solution)/shard_map/ppermute | solution.py:197
  66.2 14.4 %shard_map.71 = (bf16[40,4096]{1,0:T(8,128)(2,1)}, bf16[40,4096]{1,0:T(8,128)(2,1)}, bf16[40,4096]{1,0:T(8,128)(2,1)}, bf16[40,4096]{1,0:T(8,128)(2,1)}, bf16[40...) custom-call(bf16[1,4096,768]{2,1,0:T(8,128)(2,1)} %gate_ref.7, ...), custom_call_target="tpu_custom_call" | custom-call | flops 6039797760 | bytes 24117248 | tf_op jit(solution)/shard_map/pallas_call | solution.py:155
  83.0 10.9 %collective-permute-done.32.facts_ref = f32[16,128]{1,0:T(8,128)S(1)} collective-permute-done((f32[16,128]{1,0:T(8,128)S(1)}, f32[16,128]{1,0:T(8,128)S(1)}, u32[]{:S(2)}, u32[]{:S(2)}) %collective-permute-start.32) | collective-permute-done | bytes 8224 | tf_op jit(solution)/shard_map/ppermute | solution.py:193
  93.9 3.6 collective-permute-done.14.facts_ref
  105.0 3.1 shard_map.68
  108.2 6.0 %collective-permute-done.57.refs_3_ = bf16[40,4096]{1,0:T(8,128)(2,1)S(1)} collective-permute-done((bf16[40,4096]{1,0:T(8,128)(2,1)}, bf16[40,4096]{1,0:T(8,128)(2,1)S(1)}, u32[]{:S(2)}, u32[]{:S(2)}) %collective-permute-start.57) | collective-permute-done | bytes 327712 | tf_op jit(solution)/shard_map/ppermute | solution.py:197
  116.6 15.1 %collective-permute-done.59.refs_5_ = bf16[40,4096]{1,0:T(8,128)(2,1)S(1)} collective-permute-done((bf16[40,4096]{1,0:T(8,128)(2,1)}, bf16[40,4096]{1,0:T(8,128)(2,1)S(1)}, u32[]{:S(2)}, u32[]{:S(2)}) %collective-permute-start.59) | collective-permute-done | bytes 327712 | tf_op jit(solution)/shard_map/ppermute | solution.py:197
  136.4 4.9 %collective-permute-done.35.refs_3_ = bf16[40,4096]{1,0:T(8,128)(2,1)} collective-permute-done((bf16[40,4096]{1,0:T(8,128)(2,1)}, bf16[40,4096]{1,0:T(8,128)(2,1)}, u32[]{:S(2)}, u32[]{:S(2)}) %collective-permute-start.35) | collective-permute-done | bytes 327712 | tf_op jit(solution)/shard_map/ppermute | solution.py:197
  149.4 8.1 %collective-permute-done.36.refs_4_ = bf16[40,4096]{1,0:T(8,128)(2,1)} collective-permute-done((bf16[40,4096]{1,0:T(8,128)(2,1)}, bf16[40,4096]{1,0:T(8,128)(2,1)}, u32[]{:S(2)}, u32[]{:S(2)}) %collective-permute-start.36) | collective-permute-done | bytes 327712 | tf_op jit(solution)/shard_map/ppermute | solution.py:197
  157.5 6.4 %collective-permute-done.37.refs_5_ = bf16[40,4096]{1,0:T(8,128)(2,1)} collective-permute-done((bf16[40,4096]{1,0:T(8,128)(2,1)}, bf16[40,4096]{1,0:T(8,128)(2,1)}, u32[]{:S(2)}, u32[]{:S(2)}) %collective-permute-start.37) | collective-permute-done | bytes 327712 | tf_op jit(solution)/shard_map/ppermute | solution.py:197
  167.9 14.4 %shard_map.69 = (bf16[40,4096]{1,0:T(8,128)(2,1)}, bf16[40,4096]{1,0:T(8,128)(2,1)}, bf16[40,4096]{1,0:T(8,128)(2,1)}, bf16[40,4096]{1,0:T(8,128)(2,1)}, bf16[40...) custom-call(bf16[1,4096,768]{2,1,0:T(8,128)(2,1)} %gate_ref.7, ...), custom_call_target="tpu_custom_call" | custom-call | flops 6039797760 | bytes 24117248 | tf_op jit(solution)/shard_map/pallas_call | solution.py:155
  185.9 3.1 shard_map.66
  189.0 3.6 collective-permute-done.72.refs_8_
  195.5 4.4 %collective-permute-done.42.refs_3_ = bf16[40,4096]{1,0:T(8,128)(2,1)S(1)} collective-permute-done((bf16[40,4096]{1,0:T(8,128)(2,1)}, bf16[40,4096]{1,0:T(8,128)(2,1)S(1)}, u32[]{:S(2)}, u32[]{:S(2)}) %collective-permute-start.42) | collective-permute-done | bytes 327712 | tf_op jit(solution)/shard_map/ppermute | solution.py:197
  201.3 14.9 %collective-permute-done.44.refs_5_ = bf16[40,4096]{1,0:T(8,128)(2,1)S(1)} collective-permute-done((bf16[40,4096]{1,0:T(8,128)(2,1)}, bf16[40,4096]{1,0:T(8,128)(2,1)S(1)}, u32[]{:S(2)}, u32[]{:S(2)}) %collective-permute-start.44) | collective-permute-done | bytes 327712 | tf_op jit(solution)/shard_map/ppermute | solution.py:197
  222.2 3.1 shard_map.73
  225.4 3.1 shard_map.76
  231.6 22.9 %collective-permute-done.22.refs_5_ = bf16[40,4096]{1,0:T(8,128)(2,1)} collective-permute-done((bf16[40,4096]{1,0:T(8,128)(2,1)}, bf16[40,4096]{1,0:T(8,128)(2,1)}, u32[]{:S(2)}, u32[]{:S(2)}) %collective-permute-start.22) | collective-permute-done | bytes 327712 | tf_op jit(solution)/shard_map/ppermute | solution.py:197
  259.2 14.6 %shard_map.67 = (bf16[40,2048]{1,0:T(8,128)(2,1)}, bf16[40,2048]{1,0:T(8,128)(2,1)}, bf16[40,2048]{1,0:T(8,128)(2,1)}, bf16[40,2048]{1,0:T(8,128)(2,1)}, bf16[40...) custom-call(bf16[1,4096,768]{2,1,0:T(8,128)(2,1)} %gate_ref.7, ...), custom_call_target="tpu_custom_call" | custom-call | flops 6039797760 | bytes 24117248 | tf_op jit(solution)/shard_map/pallas_call | solution.py:155
  277.2 6.3 %collective-permute-done.73.refs_8_ = bf16[128,2048]{1,0:T(8,128)(2,1)S(1)} collective-permute-done((bf16[128,2048]{1,0:T(8,128)(2,1)}, bf16[128,2048]{1,0:T(8,128)(2,1)S(1)}, u32[]{:S(2)}, u32[]{:S(2)}) %collective-permute-start.73) | collective-permute-done | bytes 524320 | tf_op jit(solution)/shard_map/ppermute | solution.py:193
  287.8 9.4 %collective-permute-done.29.refs_5_ = bf16[40,2048]{1,0:T(8,128)(2,1)S(1)} collective-permute-done((bf16[40,2048]{1,0:T(8,128)(2,1)}, bf16[40,2048]{1,0:T(8,128)(2,1)S(1)}, u32[]{:S(2)}, u32[]{:S(2)}) %collective-permute-start.29) | collective-permute-done | bytes 163872 | tf_op jit(solution)/shard_map/ppermute | solution.py:197
  297.3 14.6 %shard_map.65 = (bf16[40,4096]{1,0:T(8,128)(2,1)}, bf16[40,4096]{1,0:T(8,128)(2,1)}, bf16[40,4096]{1,0:T(8,128)(2,1)}, bf16[40,4096]{1,0:T(8,128)(2,1)}, bf16[40...) custom-call(bf16[1,4096,768]{2,1,0:T(8,128)(2,1)} %gate_ref.7, ...), custom_call_target="tpu_custom_call" | custom-call | flops 6039797760 | bytes 24117248 | tf_op jit(solution)/shard_map/pallas_call | solution.py:155
  317.1 9.5 %collective-permute-done.68.refs_4_ = bf16[40,2048]{1,0:T(8,128)(2,1)S(1)} collective-permute-done((bf16[40,2048]{1,0:T(8,128)(2,1)S(1)}, bf16[40,2048]{1,0:T(8,128)(2,1)S(1)}, u32[]{:S(2)}, u32[]{:S(2)}) %collective-permute-start.68) | collective-permute-done | bytes 163872 | tf_op jit(solution)/shard_map/ppermute | solution.py:197
  331.5 3.1 shard_map.74
  335.3 3.1 shard_map.77
  343.3 19.2 %collective-permute-done.11.refs_5_ = bf16[40,4096]{1,0:T(8,128)(2,1)S(1)} collective-permute-done((bf16[40,4096]{1,0:T(8,128)(2,1)}, bf16[40,4096]{1,0:T(8,128)(2,1)S(1)}, u32[]{:S(2)}, u32[]{:S(2)}) %collective-permute-start.11) | collective-permute-done | bytes 327712 | tf_op jit(solution)/shard_map/ppermute | solution.py:197
  363.8 4.2 %shard_map.78 = bf16[128,4096]{1,0:T(8,128)(2,1)} custom-call(f32[16,128]{1,0:T(8,128)} %get-tuple-element.152.facts_ref, bf16[40,4096]{1,0:T(8,128)(2,1)} %get-tuple-element.85.refs_0_, bf16[40,4096]{1,0:T(8,128)(2,1)} %copy-done.20, bf16[40,4096]{1,0:T(8,128)(2,1)} %copy-done.21, bf16[40,4096]{1,0:T(8,128)(2,1)} %copy-done.22, ...), custom_call_target="tpu_custom_call" | custom-call | flops 671088640 | bytes 4718592 | tf_op jit(solution)/shard_map/pallas_call | solution.py:98
  (265 shorter events, 93.0 us)
Async XLA Ops:
  0.0 28.6 %collective-permute-start.15 = (bf16[128,4096]{1,0:T(8,128)(2,1)}, bf16[128,4096]{1,0:T(8,128)(2,1)S(1)}, u32[]{:S(2)}, u32[]{:S(2)}) collective-permute-start(bf16[128,4096]{1,0:T(8,128)(2,1)} %rows_ref.1), channel_id=1, source_target_pairs={{0,8},{1,9},{2,10},{3,11},{4,12},{5,13},{6,14},{7,15},{8,16},{9,17... | collective-permute-start | bytes 3145736 | tf_op jit(solution)/shard_map/ppermute | solution.py:193
  36.6 28.9 %collective-permute-start.52 = (bf16[40,4096]{1,0:T(8,128)(2,1)}, bf16[40,4096]{1,0:T(8,128)(2,1)S(1)}, u32[]{:S(2)}, u32[]{:S(2)}) collective-permute-start(bf16[40,4096]{1,0:T(8,128)(2,1)} %get-tuple-element.130), channel_id=1, source_target_pairs={{0,5},{1,4},{2,7},{3,6},{4,1},{5,0},{6,3},{7,2},{8,13},{9,12},{10,... | collective-permute-start | bytes 983048 | tf_op jit(solution)/shard_map/ppermute | solution.py:197
  36.8 28.7 %collective-permute-start.53 = (bf16[40,4096]{1,0:T(8,128)(2,1)}, bf16[40,4096]{1,0:T(8,128)(2,1)}, u32[]{:S(2)}, u32[]{:S(2)}) collective-permute-start(bf16[40,4096]{1,0:T(8,128)(2,1)} %get-tuple-element.131), channel_id=1, source_target_pairs={{0,6},{1,7},{2,4},{3,5},{4,2},{5,3},{6,0},{7,1},{8,14},{9,15},{10,... | collective-permute-start | bytes 983048 | tf_op jit(solution)/shard_map/ppermute | solution.py:197
  50.2 48.8 %collective-permute-start = (bf16[40,4096]{1,0:T(8,128)(2,1)}, bf16[40,4096]{1,0:T(8,128)(2,1)S(1)}, u32[]{:S(2)}, u32[]{:S(2)}) collective-permute-start(bf16[40,4096]{1,0:T(8,128)(2,1)} %get-tuple-element.78), channel_id=1, source_target_pairs={{0,1},{1,0},{2,3},{3,2},{4,5},{5,4},{6,7},{7,6},{8,9},{9,8},{10,11... | collective-permute-start | bytes 983048 | tf_op jit(solution)/shard_map/ppermute | solution.py:197
  51.2 48.5 %collective-permute-start.1 = (bf16[40,4096]{1,0:T(8,128)(2,1)}, bf16[40,4096]{1,0:T(8,128)(2,1)S(1)}, u32[]{:S(2)}, u32[]{:S(2)}) collective-permute-start(bf16[40,4096]{1,0:T(8,128)(2,1)} %get-tuple-element.79), channel_id=1, source_target_pairs={{0,2},{1,3},{2,0},{3,1},{4,6},{5,7},{6,4},{7,5},{8,10},{9,11},{10,... | collective-permute-start | bytes 983048 | tf_op jit(solution)/shard_map/ppermute | solution.py:197
  65.5 37.0 %collective-permute-start.16 = (bf16[128,4096]{1,0:T(8,128)(2,1)}, bf16[128,4096]{1,0:T(8,128)(2,1)S(1)}, u32[]{:S(2)}, u32[]{:S(2)}) collective-permute-start(bf16[128,4096]{1,0:T(8,128)(2,1)} %copy-done.44), channel_id=1, source_target_pairs={{0,8},{1,9},{2,10},{3,11},{4,12},{5,13},{6,14},{7,15},{8,16},{9,17... | collective-permute-start | bytes 3145736 | tf_op jit(solution)/shard_map/ppermute | solution.py:193
  102.0 29.7 %collective-permute-start.59 = (bf16[40,4096]{1,0:T(8,128)(2,1)}, bf16[40,4096]{1,0:T(8,128)(2,1)S(1)}, u32[]{:S(2)}, u32[]{:S(2)}) collective-permute-start(bf16[40,4096]{1,0:T(8,128)(2,1)} %get-tuple-element.138), channel_id=1, source_target_pairs={{5,0},{4,1},{7,2},{6,3},{1,4},{0,5},{3,6},{2,7},{13,8},{12,9},{15,... | collective-permute-start | bytes 983048 | tf_op jit(solution)/shard_map/ppermute | solution.py:197
  102.5 29.6 %collective-permute-start.60 = (bf16[40,4096]{1,0:T(8,128)(2,1)}, bf16[40,4096]{1,0:T(8,128)(2,1)S(1)}, u32[]{:S(2)}, u32[]{:S(2)}) collective-permute-start(bf16[40,4096]{1,0:T(8,128)(2,1)} %get-tuple-element.139), channel_id=1, source_target_pairs={{6,0},{7,1},{4,2},{5,3},{2,4},{3,5},{0,6},{1,7},{14,8},{15,9},{12,... | collective-permute-start | bytes 983048 | tf_op jit(solution)/shard_map/ppermute | solution.py:197
  108.1 24.5 %collective-permute-start.61 = (bf16[40,4096]{1,0:T(8,128)(2,1)}, bf16[40,4096]{1,0:T(8,128)(2,1)S(1)}, u32[]{:S(2)}, u32[]{:S(2)}) collective-permute-start(bf16[40,4096]{1,0:T(8,128)(2,1)} %get-tuple-element.140), channel_id=1, source_target_pairs={{7,0},{6,1},{5,2},{4,3},{3,4},{2,5},{1,6},{0,7},{15,8},{14,9},{13,... | collective-permute-start | bytes 983048 | tf_op jit(solution)/shard_map/ppermute | solution.py:197
  132.1 52.8 %collective-permute-start.17 = (bf16[128,4096]{1,0:T(8,128)(2,1)}, bf16[128,4096]{1,0:T(8,128)(2,1)S(1)}, u32[]{:S(2)}, u32[]{:S(2)}) collective-permute-start(bf16[128,4096]{1,0:T(8,128)(2,1)} %copy-done.45), channel_id=1, source_target_pairs={{0,8},{1,9},{2,10},{3,11},{4,12},{5,13},{6,14},{7,15},{8,16},{9,17... | collective-permute-start | bytes 3145736 | tf_op jit(solution)/shard_map/ppermute | solution.py:193
  132.6 24.9 %collective-permute-start.36 = (bf16[40,4096]{1,0:T(8,128)(2,1)}, bf16[40,4096]{1,0:T(8,128)(2,1)}, u32[]{:S(2)}, u32[]{:S(2)}) collective-permute-start(bf16[40,4096]{1,0:T(8,128)(2,1)} %get-tuple-element.113), channel_id=1, source_target_pairs={{0,4},{1,5},{2,6},{3,7},{4,0},{5,1},{6,2},{7,3},{8,12},{9,13},{10,... | collective-permute-start | bytes 983048 | tf_op jit(solution)/shard_map/ppermute | solution.py:197
  134.1 29.8 %collective-permute-start.37 = (bf16[40,4096]{1,0:T(8,128)(2,1)}, bf16[40,4096]{1,0:T(8,128)(2,1)}, u32[]{:S(2)}, u32[]{:S(2)}) collective-permute-start(bf16[40,4096]{1,0:T(8,128)(2,1)} %get-tuple-element.114), channel_id=1, source_target_pairs={{0,5},{1,4},{2,7},{3,6},{4,1},{5,0},{6,3},{7,2},{8,13},{9,12},{10,... | collective-permute-start | bytes 983048 | tf_op jit(solution)/shard_map/ppermute | solution.py:197
  134.6 30.8 %collective-permute-start.38 = (bf16[40,4096]{1,0:T(8,128)(2,1)}, bf16[40,4096]{1,0:T(8,128)(2,1)}, u32[]{:S(2)}, u32[]{:S(2)}) collective-permute-start(bf16[40,4096]{1,0:T(8,128)(2,1)} %get-tuple-element.115), channel_id=1, source_target_pairs={{0,6},{1,7},{2,4},{3,5},{4,2},{5,3},{6,0},{7,1},{8,14},{9,15},{10,... | collective-permute-start | bytes 983048 | tf_op jit(solution)/shard_map/ppermute | solution.py:197
  141.3 24.8 %collective-permute-start.39 = (bf16[40,4096]{1,0:T(8,128)(2,1)}, bf16[40,4096]{1,0:T(8,128)(2,1)}, u32[]{:S(2)}, u32[]{:S(2)}) collective-permute-start(bf16[40,4096]{1,0:T(8,128)(2,1)} %get-tuple-element.116), channel_id=1, source_target_pairs={{0,7},{1,6},{2,5},{3,4},{4,3},{5,2},{6,1},{7,0},{8,15},{9,14},{10,... | collective-permute-start | bytes 983048 | tf_op jit(solution)/shard_map/ppermute | solution.py:197
  157.5 24.8 %collective-permute-start.2 = (bf16[40,4096]{1,0:T(8,128)(2,1)}, bf16[40,4096]{1,0:T(8,128)(2,1)S(1)}, u32[]{:S(2)}, u32[]{:S(2)}) collective-permute-start(bf16[40,4096]{1,0:T(8,128)(2,1)} %get-tuple-element.80), channel_id=1, source_target_pairs={{0,3},{1,2},{2,1},{3,0},{4,7},{5,6},{6,5},{7,4},{8,11},{9,10},{10,... | collective-permute-start | bytes 983048 | tf_op jit(solution)/shard_map/ppermute | solution.py:197
  166.1 26.5 %collective-permute-start.72 = (bf16[128,2048]{1,0:T(8,128)(2,1)}, bf16[128,2048]{1,0:T(8,128)(2,1)S(1)}, u32[]{:S(2)}, u32[]{:S(2)}) collective-permute-start(bf16[128,2048]{1,0:T(8,128)(2,1)} %shard_map.75), channel_id=1, source_target_pairs={{0,8},{1,9},{2,10},{3,11},{4,12},{5,13},{6,14},{7,15},{8,16},{9,17... | collective-permute-start | bytes 1572872 | tf_op jit(solution)/shard_map/ppermute | solution.py:193
  192.6 23.7 %collective-permute-start.44 = (bf16[40,4096]{1,0:T(8,128)(2,1)}, bf16[40,4096]{1,0:T(8,128)(2,1)S(1)}, u32[]{:S(2)}, u32[]{:S(2)}) collective-permute-start(bf16[40,4096]{1,0:T(8,128)(2,1)} %get-tuple-element.122), channel_id=1, source_target_pairs={{5,0},{4,1},{7,2},{6,3},{1,4},{0,5},{3,6},{2,7},{13,8},{12,9},{15,... | collective-permute-start | bytes 983048 | tf_op jit(solution)/shard_map/ppermute | solution.py:197
  192.6 24.8 %collective-permute-start.45 = (bf16[40,4096]{1,0:T(8,128)(2,1)}, bf16[40,4096]{1,0:T(8,128)(2,1)S(1)}, u32[]{:S(2)}, u32[]{:S(2)}) collective-permute-start(bf16[40,4096]{1,0:T(8,128)(2,1)} %get-tuple-element.123), channel_id=1, source_target_pairs={{6,0},{7,1},{4,2},{5,3},{2,4},{3,5},{0,6},{1,7},{14,8},{15,9},{12,... | collective-permute-start | bytes 983048 | tf_op jit(solution)/shard_map/ppermute | solution.py:197
  218.0 36.5 %collective-permute-start.22 = (bf16[40,4096]{1,0:T(8,128)(2,1)}, bf16[40,4096]{1,0:T(8,128)(2,1)}, u32[]{:S(2)}, u32[]{:S(2)}) collective-permute-start(bf16[40,4096]{1,0:T(8,128)(2,1)} %get-tuple-element.98), channel_id=1, source_target_pairs={{0,5},{1,4},{2,7},{3,6},{4,1},{5,0},{6,3},{7,2},{8,13},{9,12},{10,... | collective-permute-start | bytes 983048 | tf_op jit(solution)/shard_map/ppermute | solution.py:197
  218.8 38.5 %collective-permute-start.23 = (bf16[40,4096]{1,0:T(8,128)(2,1)}, bf16[40,4096]{1,0:T(8,128)(2,1)}, u32[]{:S(2)}, u32[]{:S(2)}) collective-permute-start(bf16[40,4096]{1,0:T(8,128)(2,1)} %get-tuple-element.99), channel_id=1, source_target_pairs={{0,6},{1,7},{2,4},{3,5},{4,2},{5,3},{6,0},{7,1},{8,14},{9,15},{10,... | collective-permute-start | bytes 983048 | tf_op jit(solution)/shard_map/ppermute | solution.py:197
  222.2 36.5 %collective-permute-start.24 = (bf16[40,4096]{1,0:T(8,128)(2,1)}, bf16[40,4096]{1,0:T(8,128)(2,1)}, u32[]{:S(2)}, u32[]{:S(2)}) collective-permute-start(bf16[40,4096]{1,0:T(8,128)(2,1)} %get-tuple-element.100), channel_id=1, source_target_pairs={{0,7},{1,6},{2,5},{3,4},{4,3},{5,2},{6,1},{7,0},{8,15},{9,14},{10,... | collective-permute-start | bytes 983048 | tf_op jit(solution)/shard_map/ppermute | solution.py:197
  228.5 45.2 %collective-permute-start.4 = (bf16[40,4096]{1,0:T(8,128)(2,1)}, bf16[40,4096]{1,0:T(8,128)(2,1)S(1)}, u32[]{:S(2)}, u32[]{:S(2)}) collective-permute-start(bf16[40,4096]{1,0:T(8,128)(2,1)} %get-tuple-element.82), channel_id=1, source_target_pairs={{0,5},{1,4},{2,7},{3,6},{4,1},{5,0},{6,3},{7,2},{8,13},{9,12},{10,... | collective-permute-start | bytes 983048 | tf_op jit(solution)/shard_map/ppermute | solution.py:197
  229.9 43.9 %collective-permute-start.5 = (bf16[40,4096]{1,0:T(8,128)(2,1)}, bf16[40,4096]{1,0:T(8,128)(2,1)S(1)}, u32[]{:S(2)}, u32[]{:S(2)}) collective-permute-start(bf16[40,4096]{1,0:T(8,128)(2,1)} %get-tuple-element.83), channel_id=1, source_target_pairs={{0,6},{1,7},{2,4},{3,5},{4,2},{5,3},{6,0},{7,1},{8,14},{9,15},{10,... | collective-permute-start | bytes 983048 | tf_op jit(solution)/shard_map/ppermute | solution.py:197
  258.7 24.8 %collective-permute-start.73 = (bf16[128,2048]{1,0:T(8,128)(2,1)}, bf16[128,2048]{1,0:T(8,128)(2,1)S(1)}, u32[]{:S(2)}, u32[]{:S(2)}) collective-permute-start(bf16[128,2048]{1,0:T(8,128)(2,1)} %shard_map.76), channel_id=1, source_target_pairs={{0,8},{1,9},{2,10},{3,11},{4,12},{5,13},{6,14},{7,15},{8,16},{9,17... | collective-permute-start | bytes 1572872 | tf_op jit(solution)/shard_map/ppermute | solution.py:193
  284.1 27.8 %collective-permute-start.30 = (bf16[40,2048]{1,0:T(8,128)(2,1)}, bf16[40,2048]{1,0:T(8,128)(2,1)S(1)}, u32[]{:S(2)}, u32[]{:S(2)}) collective-permute-start(bf16[40,2048]{1,0:T(8,128)(2,1)} %get-tuple-element.107), channel_id=1, source_target_pairs={{6,0},{7,1},{4,2},{5,3},{2,4},{3,5},{0,6},{1,7},{14,8},{15,9},{12,... | collective-permute-start | bytes 491528 | tf_op jit(solution)/shard_map/ppermute | solution.py:197
  284.8 27.6 %collective-permute-start.31 = (bf16[40,2048]{1,0:T(8,128)(2,1)}, bf16[40,2048]{1,0:T(8,128)(2,1)S(1)}, u32[]{:S(2)}, u32[]{:S(2)}) collective-permute-start(bf16[40,2048]{1,0:T(8,128)(2,1)} %get-tuple-element.108), channel_id=1, source_target_pairs={{7,0},{6,1},{5,2},{4,3},{3,4},{2,5},{1,6},{0,7},{15,8},{14,9},{13,... | collective-permute-start | bytes 491528 | tf_op jit(solution)/shard_map/ppermute | solution.py:197
  287.4 26.5 %collective-permute-start.65 = (bf16[40,2048]{1,0:T(8,128)(2,1)}, bf16[40,2048]{1,0:T(8,128)(2,1)S(1)}, u32[]{:S(2)}, u32[]{:S(2)}) collective-permute-start(bf16[40,2048]{1,0:T(8,128)(2,1)} %get-tuple-element.142), channel_id=1, source_target_pairs={{1,0},{0,1},{3,2},{2,3},{5,4},{4,5},{7,6},{6,7},{9,8},{8,9},{11,10... | collective-permute-start | bytes 491528 | tf_op jit(solution)/shard_map/ppermute | solution.py:197
  287.4 26.6 %collective-permute-start.66 = (bf16[40,2048]{1,0:T(8,128)(2,1)}, bf16[40,2048]{1,0:T(8,128)(2,1)S(1)}, u32[]{:S(2)}, u32[]{:S(2)}) collective-permute-start(bf16[40,2048]{1,0:T(8,128)(2,1)} %get-tuple-element.143), channel_id=1, source_target_pairs={{2,0},{3,1},{0,2},{1,3},{6,4},{7,5},{4,6},{5,7},{10,8},{11,9},{8,1... | collective-permute-start | bytes 491528 | tf_op jit(solution)/shard_map/ppermute | solution.py:197
  312.0 26.5 %collective-permute-start.7 = (bf16[40,4096]{1,0:T(8,128)(2,1)}, bf16[40,4096]{1,0:T(8,128)(2,1)S(1)}, u32[]{:S(2)}, u32[]{:S(2)}) collective-permute-start(bf16[40,4096]{1,0:T(8,128)(2,1)} %get-tuple-element.86), channel_id=1, source_target_pairs={{1,0},{0,1},{3,2},{2,3},{5,4},{4,5},{7,6},{6,7},{9,8},{8,9},{11,10... | collective-permute-start | bytes 983048 | tf_op jit(solution)/shard_map/ppermute | solution.py:197
  334.7 27.9 %collective-permute-start.64 = (bf16[128,2048]{1,0:T(8,128)(2,1)}, bf16[128,2048]{1,0:T(8,128)(2,1)S(1)}, u32[]{:S(2)}, u32[]{:S(2)}) collective-permute-start(bf16[128,2048]{1,0:T(8,128)(2,1)} %shard_map.74), channel_id=1, source_target_pairs={{0,8},{1,9},{2,10},{3,11},{4,12},{5,13},{6,14},{7,15},{8,16},{9,17... | collective-permute-start | bytes 1572872 | tf_op jit(solution)/shard_map/ppermute | solution.py:193
  338.5 24.1 %collective-permute-start.74 = (bf16[128,2048]{1,0:T(8,128)(2,1)}, bf16[128,2048]{1,0:T(8,128)(2,1)S(1)}, u32[]{:S(2)}, u32[]{:S(2)}) collective-permute-start(bf16[128,2048]{1,0:T(8,128)(2,1)} %shard_map.77), channel_id=1, source_target_pairs={{0,8},{1,9},{2,10},{3,11},{4,12},{5,13},{6,14},{7,15},{8,16},{9,17... | collective-permute-start | bytes 1572872 | tf_op jit(solution)/shard_map/ppermute | solution.py:193
  338.5 24.0 %collective-permute-start.11 = (bf16[40,4096]{1,0:T(8,128)(2,1)}, bf16[40,4096]{1,0:T(8,128)(2,1)S(1)}, u32[]{:S(2)}, u32[]{:S(2)}) collective-permute-start(bf16[40,4096]{1,0:T(8,128)(2,1)} %get-tuple-element.90), channel_id=1, source_target_pairs={{5,0},{4,1},{7,2},{6,3},{1,4},{0,5},{3,6},{2,7},{13,8},{12,9},{15,... | collective-permute-start | bytes 983048 | tf_op jit(solution)/shard_map/ppermute | solution.py:197
  (106 other events, 1712.4 us)
